TPU v7x, 128 devices: a whole 4x4x4 slice. The times are simulated.
128 devices in a mesh: grp: 2 (over core), seg: 64 (over x, y, z).
Axes of the slice: x: 4, y: 4, z: 4, core: 2. Of those that a mesh axis runs over, the one named last changes fastest.
Arguments:
- coeffs: bfloat16 [858, 32768], P(None, ('grp', 'seg')), may hold values from -6 to 6
- tracer: bfloat16 [286, 32768], P(None, ('grp', 'seg')), may hold values from -6 to 6
- up_op: bfloat16 [168, 858], replicated, may hold values from -0.21875 to 0.21875
- far_ops: bfloat16 [168, 16, 168], replicated, may hold values from -0.005859375 to 0.005859375
- down_op: bfloat16 [858, 168], replicated, may hold values from -0.5 to 0.5
- near_ops: bfloat16 [858, 8, 858], replicated, may hold values from -0.0390625 to 0.0390625
- face_dirs: float32 [3, 8], replicated, may hold values from -4 to 4
- leaf_octant: int32 [32768], P(('grp', 'seg')), may hold values from 0 to 1023, as said below
- far_src: int32 [189, 1024], P(None, ('grp', 'seg')), may hold values from 0 to 1023
- far_type: int32 [189, 1024], P(None, ('grp', 'seg')), may hold values from 0 to 15
- near_list: int32 [27, 32768], P(None, ('grp', 'seg')), may hold values from 0 to 511, as said below
- near_type: int32 [27, 32768], P(None, ('grp', 'seg')), may hold values from 0 to 8, as said below
- new_owner: int32 [32768, 1], P(('grp', 'seg')), may hold values from 0 to 127; in each aligned block of 256 rows (0 to 255, 256 to 511, ...) at most 4 rows name the same one
Outputs:
- moved: bfloat16 [1144, 65536], P(None, ('grp', 'seg'))
Inputs may be any that keep to these rules, and one draw needn't show every extreme that they name: `leaf_octant`: never falling along the leaves; every octant holds at least one leaf; octant o begins at leaf 0 for o = 0, else among the 32 leaves that end at leaf o * 32. neighbour[k, l] = (l // 256) * 256 - 128 + near_list[k, l] is a leaf of the same group of devices along seg as leaf l. `near_type`: the value 8 marks an empty slot. `new_owner`: among the 256 leaves of one device, at most 4 have the same new owner.
All inputs are finite; a program needn't handle non-finite values.
Results may differ from a plain program's by a relative error of at most 0.0065.
Values may be sent and summed in bfloat16 or wider, within the bound.
A program may use at most 128 MiB of HBM per device.

v0:
```python
import jax
import jax.numpy as jnp
from jax import lax
from jax.sharding import Mesh
from jax.sharding import PartitionSpec as P

NCOEF = 286
HALO = 128
SEG = ("seg_0", "seg_1", "seg_2")
GRP_SEG = ("grp", "seg_0", "seg_1", "seg_2")


def sum_by_axis(array, axes, dim):
    if not axes:
        return array
    nearer = lax.psum_scatter(array, axes[0], scatter_dimension=dim, tiled=True)
    return sum_by_axis(nearer, axes[1:], dim)


def in_order(blocks, dim):
    blocks = jnp.moveaxis(blocks, 0, dim)
    shape = blocks.shape
    return blocks.reshape(*shape[:dim], shape[dim] * shape[dim + 1], *shape[dim + 2 :])


def stacked_from(array, axes, sequence):
    blocks = array[None]
    for k in sequence:
        blocks = lax.all_gather(blocks, axes[k], axis=0, tiled=True)
    block = [lax.axis_size(axes[k]) for k in reversed(sequence)]
    blocks = blocks.reshape(*block, *array.shape)
    turned = sorted(range(len(sequence)), key=lambda place: sequence[len(sequence) - 1 - place])
    return blocks.transpose(*turned, *range(len(sequence), blocks.ndim)).reshape(-1, *array.shape)


def gather_axes(array, axes, sequence, dim):
    return in_order(stacked_from(array, axes, sequence), dim)


def extended(array, sides, width):
    for axis, dim in sides:
        devices, length = (lax.axis_size(axis), array.shape[dim])
        up = [(i, (i + 1) % devices) for i in range(devices - 1)]
        down = [(j, i) for i, j in up]
        last = lax.slice_in_dim(array, length - width, length, axis=dim)
        initial = lax.slice_in_dim(array, 0, width, axis=dim)
        before = lax.ppermute(last, axis, up)
        after = lax.ppermute(initial, axis, down)
        array = jnp.concatenate([before, array, after], axis=dim)
    return array


def octant_column(octant, per_device, devices):
    block = octant // per_device
    owner = jnp.where(block % 2 == 1, block - 1, (block - devices // 2 - 1) % devices)
    return owner * per_device + octant % per_device


def local(
    coeffs,
    tracer,
    up_op,
    far_ops,
    down_op,
    near_ops,
    face_dirs,
    leaf_octant,
    far_src,
    far_type,
    near_list,
    near_type,
    new_owner,
):
    leaves = coeffs.shape[1]
    coef_rows = coeffs.shape[0]
    pole_rows = up_op.shape[0]
    far_kinds = far_ops.shape[1]
    near_kinds = near_ops.shape[1]
    slot_count = near_list.shape[0]
    far_slots = far_src.shape[0]
    own_octants = far_src.shape[1]
    group_count = lax.axis_size("grp")
    segment_count = lax.axis_size(SEG)
    devices = group_count * segment_count
    octants = own_octants * devices
    leaf_column = octant_column(leaf_octant, own_octants, devices)
    leaf_pole = jnp.dot(up_op, coeffs, preferred_element_type=jnp.float32).astype(jnp.bfloat16)
    octant_hot = (leaf_column[:, None] == jnp.arange(octants, dtype=jnp.int32)[None, :]).astype(
        jnp.bfloat16
    )
    partial_value = jnp.dot(leaf_pole, octant_hot, preferred_element_type=jnp.float32)
    own_pole = sum_by_axis(partial_value, GRP_SEG, 1).astype(jnp.bfloat16)
    all_pole = gather_axes(own_pole, GRP_SEG, (1, 2, 3, 0), 1)
    source_column = octant_column(far_src, own_octants, devices)
    target_index = far_type * own_octants + jnp.arange(own_octants, dtype=jnp.int32)[None, :]
    octant_iota = jnp.arange(octants, dtype=jnp.int32)
    target_iota = jnp.arange(far_kinds * own_octants, dtype=jnp.int32)

    def add_far(slot_index, running):
        source_hot = (octant_iota[:, None] == source_column[slot_index][None, :]).astype(
            jnp.float32
        )
        target_hot = (target_iota[None, :] == target_index[slot_index][:, None]).astype(jnp.float32)
        return running + jnp.dot(source_hot, target_hot, precision=lax.Precision.HIGHEST)

    far_count = lax.fori_loop(
        0, far_slots, add_far, jnp.zeros((octants, far_kinds * own_octants), jnp.float32)
    ).astype(jnp.bfloat16)
    grouped = jnp.dot(all_pole, far_count, preferred_element_type=jnp.float32).astype(jnp.bfloat16)
    grouped = jnp.transpose(grouped.reshape(pole_rows, far_kinds, own_octants), (1, 0, 2))
    own_local = jnp.dot(
        far_ops.reshape(pole_rows, far_kinds * pole_rows),
        grouped.reshape(far_kinds * pole_rows, own_octants),
        preferred_element_type=jnp.float32,
    ).astype(jnp.bfloat16)
    shard_part = gather_axes(own_local, GRP_SEG, (1, 2, 3, 0), 1)
    piece_width = shard_part.shape[1]
    chooser = (leaf_column[None, :] == jnp.arange(piece_width, dtype=jnp.int32)[:, None]).astype(
        jnp.bfloat16
    )
    leaf_local = jnp.dot(shard_part, chooser, preferred_element_type=jnp.float32).astype(
        jnp.bfloat16
    )
    far_field = jnp.dot(down_op, leaf_local, preferred_element_type=jnp.float32)
    flat_ops = near_ops.reshape(coef_rows * near_kinds, coef_rows)
    window = extended(coeffs, ((SEG, 1),), HALO)
    images = jnp.dot(flat_ops, window, preferred_element_type=jnp.float32).astype(jnp.bfloat16)
    window_span = images.shape[1]
    images = images.reshape(coef_rows, near_kinds * window_span)
    live_slot = near_type < near_kinds
    kind_index = jnp.clip(near_type, 0, near_kinds - 1)
    combined = jnp.where(live_slot, kind_index * window_span + near_list, -1)
    image_iota = jnp.arange(near_kinds * window_span, dtype=jnp.int32)

    def count_slot(slot_index, running):
        return running + (image_iota[:, None] == combined[slot_index][None, :]).astype(jnp.float32)

    selection = lax.fori_loop(
        0, slot_count, count_slot, jnp.zeros((near_kinds * window_span, leaves), jnp.float32)
    ).astype(jnp.bfloat16)
    near_field = jnp.dot(images, selection, preferred_element_type=jnp.float32)
    velocity = near_field + far_field
    speeds = velocity[::NCOEF]
    normal_speed = (
        face_dirs[0][:, None] * speeds[0][None, :]
        + face_dirs[1][:, None] * speeds[1][None, :]
        + face_dirs[2][:, None] * speeds[2][None, :]
    )
    inflow = jnp.where(
        live_slot, jnp.maximum(jnp.take_along_axis(normal_speed, kind_index, axis=0), 0.0), 0.0
    )
    denominator = 1.0 + jnp.sum(inflow, axis=0)
    weights = inflow / denominator[None, :]
    retained = 1.0 - jnp.sum(weights, axis=0)
    tracer_window = extended(tracer, ((SEG, 1),), HALO)
    tracer_span = tracer_window.shape[1]
    place_iota = jnp.arange(tracer_span, dtype=jnp.int32)

    def weigh_slot(slot_index, running):
        hits = place_iota[:, None] == near_list[slot_index][None, :]
        return running + jnp.where(hits, weights[slot_index][None, :], jnp.zeros((), jnp.float32))

    mixing = lax.fori_loop(0, slot_count, weigh_slot, jnp.zeros((tracer_span, leaves), jnp.float32))
    incoming = jnp.dot(tracer_window.astype(jnp.float32), mixing, precision=lax.Precision.HIGHEST)
    blended = tracer.astype(jnp.float32) * retained[None, :] + incoming
    payload = jnp.concatenate([velocity.astype(jnp.bfloat16), blended.astype(jnp.bfloat16)], axis=0)
    capacity = max(2, 2 * leaves // devices)
    owner_column = new_owner[:, 0]
    owner_hot = (owner_column[:, None] == jnp.arange(devices, dtype=jnp.int32)[None, :]).astype(
        jnp.int32
    )
    slot_rank = jnp.sum(jnp.cumsum(owner_hot, axis=0) * owner_hot, axis=1) - 1
    slot_place = owner_column * capacity + slot_rank
    placement = (
        slot_place[:, None] == jnp.arange(devices * capacity, dtype=jnp.int32)[None, :]
    ).astype(jnp.bfloat16)
    outgoing = jnp.dot(payload, placement, preferred_element_type=jnp.float32).astype(jnp.bfloat16)
    payload_rows = outgoing.shape[0]
    blocked = outgoing.reshape(payload_rows, group_count, segment_count, capacity)
    arriving = lax.all_to_all(
        lax.all_to_all(blocked, SEG, split_axis=2, concat_axis=2, tiled=True),
        "grp",
        split_axis=1,
        concat_axis=1,
        tiled=True,
    )
    moved = arriving.reshape(payload_rows, devices * capacity)
    return moved


def solution(mesh):
    torus = Mesh(
        mesh.devices.reshape(mesh.shape["grp"], 4, 4, 4), ("grp", "seg_0", "seg_1", "seg_2")
    )
    in_specs = (
        P(None, GRP_SEG),
        P(None, GRP_SEG),
        P(),
        P(),
        P(),
        P(),
        P(),
        P(GRP_SEG),
        P(None, GRP_SEG),
        P(None, GRP_SEG),
        P(None, GRP_SEG),
        P(None, GRP_SEG),
        P(GRP_SEG, None),
    )
    out_specs = P(None, GRP_SEG)
    return jax.shard_map(local, mesh=torus, in_specs=in_specs, out_specs=out_specs, check_vma=False)
```

profile of v0, /device:TPU:1, one launch (start us, length us, event | category | flops | bytes accessed | tf_op | source)
XLA Modules:
  0.0 483.4 jit_solution(2065656241753058865)
XLA Ops:
  6.5 1.9 fusion.74
  8.5 1.3 collective-permute-start.1
  9.8 5.7 %collective-permute-start = (bf16[858,128]{1,0:T(8,128)(2,1)}, bf16[858,128]{1,0:T(8,128)(2,1)}, u32[]{:S(2)}, u32[]{:S(2)}) collective-permute-start(bf16[858,128]{1,0:T(8,128)(2,1)} %get-tuple-element.366), channel_id=1, source_target_pairs={{0,1},{1,2},{2,3},{3,4},{4,5},{5,6},{6,7},{7,8},{8,9},{9,10},{10,1... | collective-permute-start | bytes 658952 | tf_op jit(solution)/shard_map/ppermute | solution.py:47
  16.2 2.5 fusion.24
  18.8 1.6 fusion.75
  20.4 1.3 collective-permute-start.3
  21.7 4.0 collective-permute-start.2
  25.7 0.8 copy.56
  27.5 71.3 %while.43 = (s32[]{:T(128)}, f32[1024,128]{1,0:T(8,128)S(1)}, s32[189,8]{1,0:T(8,128)S(1)}, s32[189,8]{1,0:T(8,128)S(1)}, s32[]{:T(128)}, /*index=5*/s32[]{:T(128)}) while((s32[]{:T(128)}, f32[1024,128]{1,0:T(8,128)S(1)}, s32[189,8]{1,0:T(8,128)S(1)}, s32[189,8]{1,0:T(8,128)S(1)}, s32[]{:T(128)}, /*index=5*/s32[]{:T(128)}) %tuple.101), condition=%wide.region_7.8_spmd.clone, body=%wide.region_6.7_spmd.clone.sunk | while | flops 2368515 | bytes 1048859 | solution.py:106
  98.9 128.0 %while.42 = (s32[]{:T(128)}, f32[4096,256]{1,0:T(8,128)}, s32[27,256]{1,0:T(8,128)S(1)}, s32[]{:T(128)}, s32[]{:T(128)}) while((s32[]{:T(128)}, f32[4096,256]{1,0:T(8,128)}, s32[27,256]{1,0:T(8,128)S(1)}, s32[]{:T(128)}, s32[]{:T(128)}) %tuple.98), condition=%wide.region_1.2_spmd.clone, body=%wide.region_0.1_spmd.clone.sunk | while | flops 4194307 | bytes 8391763 | solution.py:138
  98.9 2.6 select_add_fusion.4
  101.5 4.8 select_add_fusion.4
  106.3 4.8 select_add_fusion.4
  111.2 4.8 select_add_fusion.4
  116.0 4.8 select_add_fusion.4
  120.8 4.8 select_add_fusion.4
  125.6 4.8 select_add_fusion.4
  130.4 4.8 select_add_fusion.4
  135.3 4.8 select_add_fusion.4
  140.1 4.8 select_add_fusion.4
  144.9 4.8 select_add_fusion.4
  149.7 4.8 select_add_fusion.4
  154.5 4.8 select_add_fusion.4
  159.4 4.8 select_add_fusion.4
  164.2 4.8 select_add_fusion.4
  169.0 4.8 select_add_fusion.4
  173.8 4.8 select_add_fusion.4
  178.6 4.8 select_add_fusion.4
  183.5 4.8 select_add_fusion.4
  188.3 4.8 select_add_fusion.4
  193.1 4.8 select_add_fusion.4
  197.9 4.8 select_add_fusion.4
  202.7 4.8 select_add_fusion.4
  207.5 4.8 select_add_fusion.4
  212.4 4.8 select_add_fusion.4
  217.2 4.8 select_add_fusion.4
  222.0 4.8 select_add_fusion.4
  228.8 28.3 %reduce-scatter.11.cloned.1.call-done = f32[168,128]{1,0:T(8,128)} async-done(((f32[168,512]{1,0:T(8,128)}), f32[168,128]{1,0:T(8,128)}) %reduce-scatter.11.cloned.1.call-update) | async-done | bytes 86032 | tf_op jit(solution)/shard_map/reduce_scatter | solution.py:16
  257.0 1.6 copy.71
  258.8 12.3 %fusion.15 = bf16[6864,512]{1,0:T(8,128)(2,1)} fusion(bf16[858,8,858]{2,1,0:T(8,128)(2,1)} %param.24, bf16[858,128]{1,0:T(8,128)(2,1)} %collective-permute-done.1, bf16[858,256]{1,0:T(8,128)(2,1)S(1)} %copy-done.1, bf16[858,128]{1,0:T(8,128)(2,1)} %collective-permute-done), kind=kOutput, calls=%fused_computation.22 | convolution fusion | flops 6036805632 | bytes 19685952 | tf_op jit(solution)/shard_map/dot_general | solution.py:127
  271.1 11.7 %reshape.86 = bf16[858,4096]{1,0:T(8,128)(2,1)} reshape(bf16[6864,512]{1,0:T(8,128)(2,1)} %fusion.15) | data formatting | bytes 14057472 | tf_op jit(solution)/shard_map/reshape | solution.py:129
  282.8 7.1 %fusion.18 = f32[858,256]{1,0:T(8,128)} fusion(bf16[858,4096]{1,0:T(8,128)(2,1)} %reshape.86, f32[4096,256]{1,0:T(8,128)} %get-tuple-element.287), kind=kOutput, calls=%fused_computation.24 | convolution fusion | flops 1800404992 | bytes 12101632 | tf_op jit(solution)/shard_map/dot_general | solution.py:141
  289.9 13.6 %reduce-scatter.15.cloned.1.call-done = f32[8,168]{1,0:T(8,128)} async-done(((f32[32,168]{1,0:T(8,128)}), f32[8,168]{1,0:T(8,128)}) %reduce-scatter.15.cloned.1.call-update) | async-done | bytes 5392
  303.5 0.8 copy.74
  304.4 9.5 %all-gather.2 = bf16[4,168,8]{1,2,0:T(8,128)(2,1)S(1)} all-gather(bf16[1,168,8]{1,2,0:T(8,128)(2,1)S(1)} %copy.54), channel_id=2, replica_groups=mesh['grp'=2,'seg_0'=4,'seg_1'=4,'seg_2'=4] {'seg_0'}, dimensions={0}, use_global_device_ids=true | all-gather | bytes 13440 | tf_op jit(solution)/shard_map/all_gather | solution.py:29
  313.8 9.3 %all_gather.25 = bf16[16,168,8]{1,2,0:T(8,128)(2,1)S(1)} all-gather(bf16[4,168,8]{1,2,0:T(8,128)(2,1)S(1)} %all-gather.2), channel_id=1, replica_groups=mesh['grp'=2,'seg_0'=4,'seg_1'=4,'seg_2'=4] {'seg_1'}, dimensions={0}, use_global_device_ids=true | all-gather | bytes 53760 | tf_op jit(solution)/shard_map/all_gather | solution.py:29
  323.1 9.4 %all_gather.26 = bf16[64,168,8]{1,2,0:T(8,128)(2,1)S(1)} all-gather(bf16[16,168,8]{1,2,0:T(8,128)(2,1)S(1)} %all_gather.25), channel_id=1, replica_groups=mesh['grp'=2,'seg_0'=4,'seg_1'=4,'seg_2'=4] {'seg_2'}, dimensions={0}, use_global_device_ids=true | all-gather | bytes 215040 | tf_op jit(solution)/shard_map/all_gather | solution.py:29
  332.5 13.4 %all_gather.27 = bf16[128,168,8]{1,2,0:T(8,128)(2,1)S(1)} all-gather(bf16[64,168,8]{1,2,0:T(8,128)(2,1)S(1)} %all_gather.26), channel_id=1, replica_groups=mesh['grp'=2,'seg_0'=4,'seg_1'=4,'seg_2'=4] {'grp'}, dimensions={0}, use_global_device_ids=true | all-gather | bytes 516096 | tf_op jit(solution)/shard_map/all_gather | solution.py:29
  346.4 0.8 fusion.31
  347.3 9.1 %all-gather.3 = bf16[4,168,8]{1,2,0:T(8,128)(2,1)S(1)} all-gather(bf16[1,168,8]{1,2,0:T(8,128)(2,1)S(1)} %fusion.31), channel_id=3, replica_groups=mesh['grp'=2,'seg_0'=4,'seg_1'=4,'seg_2'=4] {'seg_0'}, dimensions={0}, use_global_device_ids=true | all-gather | bytes 13440 | tf_op jit(solution)/shard_map/all_gather | solution.py:29
  356.4 9.0 %all_gather.29 = bf16[16,168,8]{1,2,0:T(8,128)(2,1)S(1)} all-gather(bf16[4,168,8]{1,2,0:T(8,128)(2,1)S(1)} %all-gather.3), channel_id=1, replica_groups=mesh['grp'=2,'seg_0'=4,'seg_1'=4,'seg_2'=4] {'seg_1'}, dimensions={0}, use_global_device_ids=true | all-gather | bytes 53760 | tf_op jit(solution)/shard_map/all_gather | solution.py:29
  365.4 9.4 %all_gather.30 = bf16[64,168,8]{1,2,0:T(8,128)(2,1)S(1)} all-gather(bf16[16,168,8]{1,2,0:T(8,128)(2,1)S(1)} %all_gather.29), channel_id=1, replica_groups=mesh['grp'=2,'seg_0'=4,'seg_1'=4,'seg_2'=4] {'seg_2'}, dimensions={0}, use_global_device_ids=true | all-gather | bytes 215040 | tf_op jit(solution)/shard_map/all_gather | solution.py:29
  374.7 11.0 %all_gather.31 = bf16[128,168,8]{1,2,0:T(8,128)(2,1)S(1)} all-gather(bf16[64,168,8]{1,2,0:T(8,128)(2,1)S(1)} %all_gather.30), channel_id=1, replica_groups=mesh['grp'=2,'seg_0'=4,'seg_1'=4,'seg_2'=4] {'grp'}, dimensions={0}, use_global_device_ids=true | all-gather | bytes 516096 | tf_op jit(solution)/shard_map/all_gather | solution.py:29
  385.8 2.7 fusion.77
  389.3 38.3 %gather_fusion = f32[6912]{0:T(1024)S(1)} fusion(f32[8,256]{1,0:T(8,128)S(1)} %multiply_add_fusion, s32[6912]{0:T(1024)S(1)} %reshape.98), kind=kCustom, calls=%fused_computation | custom fusion | bytes 110592 | tf_op jit(solution)/shard_map/jit(take_along_axis)/gather | solution.py:150
  427.8 5.9 %while.44 = (s32[]{:T(128)}, f32[512,256]{1,0:T(8,128)S(1)}, s32[27,256]{1,0:T(8,128)S(1)}, f32[27,256]{1,0:T(8,128)S(1)}, s32[]{:T(128)}, /*index=5*/s32[]{:T(128)}) while((s32[]{:T(128)}, f32[512,256]{1,0:T(8,128)S(1)}, s32[27,256]{1,0:T(8,128)S(1)}, f32[27,256]{1,0:T(8,128)S(1)}, s32[]{:T(128)}, /*index=5*/s32[]{:T(128)}) %tuple.115), condition=%wide.region_11.12_spmd.clone, body=%wide.region_10.11_spmd.clone.sunk | while | flops 524291 | bytes 1054815 | solution.py:163
  434.2 1.6 convolution_convert_fusion
  435.8 1.7 copy.67
  437.5 1.2 reshape.96
  438.7 1.7 copy.68
  440.4 25.2 %all_to_all.10 = bf16[1144,2,64,4]{0,3,1,2:T(4,128)(2,1)S(1)} all-to-all(bf16[1144,2,64,4]{0,3,1,2:T(4,128)(2,1)S(1)} %copy.68), channel_id=1, replica_groups=mesh['grp'=2,'seg_0'=4,'seg_1'=4,'seg_2'=4] {'seg_0','seg_1','seg_2'}, dimensions={2} | all-to-all | bytes 2342912 | tf_op jit(solution)/shard_map/all_to_all | solution.py:181
  466.0 7.1 %all_to_all.11 = bf16[1144,2,64,4]{0,3,2,1:T(4,128)(2,1)S(1)} all-to-all(bf16[1144,2,64,4]{0,3,2,1:T(4,128)(2,1)S(1)} %copy.69), channel_id=1, replica_groups=mesh['grp'=2,'seg_0'=4,'seg_1'=4,'seg_2'=4] {'grp'}, dimensions={1} | all-to-all | bytes 2342912 | tf_op jit(solution)/shard_map/all_to_all | solution.py:180
  473.1 1.4 reshape.97
  474.5 2.4 copy.70
  (555 shorter events, 75.8 us)
Async XLA Ops:
  6.5 339.9 %copy-start = (bf16[168,16,168]{2,1,0:T(8,128)(2,1)S(1)}, bf16[168,16,168]{2,1,0:T(8,128)(2,1)}, u32[]{:S(2)}) copy-start(bf16[168,16,168]{2,1,0:T(8,128)(2,1)} %param.22) | copy-start | bytes 2709508
  6.5 220.7 %reduce-scatter.9.cloned.1.call-start = ((), (), s32[]{:S(2)}) async-start(), calls=%async_computation.6 | async-start | bytes 1032192 | tf_op jit(solution)/shard_map/reduce_scatter | solution.py:16
  8.5 250.3 %collective-permute-start.1 = (bf16[858,128]{1,0:T(8,128)(2,1)}, bf16[858,128]{1,0:T(8,128)(2,1)}, u32[]{:S(2)}, u32[]{:S(2)}) collective-permute-start(bf16[858,128]{1,0:T(8,128)(2,1)} %get-tuple-element.367), channel_id=1, source_target_pairs={{1,0},{2,1},{3,2},{4,3},{5,4},{6,5},{7,6},{8,7},{9,8},{10,9},{11,1... | collective-permute-start | bytes 658952 | tf_op jit(solution)/shard_map/ppermute | solution.py:48
  9.8 249.0 %collective-permute-start = (bf16[858,128]{1,0:T(8,128)(2,1)}, bf16[858,128]{1,0:T(8,128)(2,1)}, u32[]{:S(2)}, u32[]{:S(2)}) collective-permute-start(bf16[858,128]{1,0:T(8,128)(2,1)} %get-tuple-element.366), channel_id=1, source_target_pairs={{0,1},{1,2},{2,3},{3,4},{4,5},{5,6},{6,7},{7,8},{8,9},{9,10},{10,1... | collective-permute-start | bytes 658952 | tf_op jit(solution)/shard_map/ppermute | solution.py:47
  18.7 80.1 %copy-start.3 = (s32[27,256]{1,0:T(8,128)S(1)}, s32[27,256]{1,0:T(8,128)}, u32[]{:S(2)}) copy-start(s32[27,256]{1,0:T(8,128)} %param.30) | copy-start | bytes 82948
  18.7 80.1 %copy-start.5 = (s32[27,256]{1,0:T(8,128)S(1)}, s32[27,256]{1,0:T(8,128)}, u32[]{:S(2)}) copy-start(s32[27,256]{1,0:T(8,128)} %param.29) | copy-start | bytes 82948
  18.7 238.3 %reduce-scatter.11.cloned.1.call-start = ((), (), s32[]{:S(2)}) async-start(), calls=%async_computation.7 | async-start | bytes 430080 | tf_op jit(solution)/shard_map/reduce_scatter | solution.py:16
  20.4 413.4 %collective-permute-start.3 = (bf16[286,128]{1,0:T(8,128)(2,1)}, bf16[286,128]{1,0:T(8,128)(2,1)S(1)}, u32[]{:S(2)}, u32[]{:S(2)}) collective-permute-start(bf16[286,128]{1,0:T(8,128)(2,1)} %get-tuple-element.369), channel_id=1, source_target_pairs={{1,0},{2,1},{3,2},{4,3},{5,4},{6,5},{7,6},{8,7},{9,8},{10,9},{11,1... | collective-permute-start | bytes 219656 | tf_op jit(solution)/shard_map/ppermute | solution.py:48
  21.7 412.1 %collective-permute-start.2 = (bf16[286,128]{1,0:T(8,128)(2,1)}, bf16[286,128]{1,0:T(8,128)(2,1)S(1)}, u32[]{:S(2)}, u32[]{:S(2)}) collective-permute-start(bf16[286,128]{1,0:T(8,128)(2,1)} %get-tuple-element.368), channel_id=1, source_target_pairs={{0,1},{1,2},{2,3},{3,4},{4,5},{5,6},{6,7},{7,8},{8,9},{9,10},{10,1... | collective-permute-start | bytes 219656 | tf_op jit(solution)/shard_map/ppermute | solution.py:47
  98.8 128.0 %copy-start.6 = (s32[256,1]{0,1:T(1,128)S(1)}, s32[256,1]{0,1:T(1,128)}, u32[]{:S(2)}) copy-start(s32[256,1]{0,1:T(1,128)} %param.31) | copy-start | bytes 3076
  98.8 128.7 %copy-start.7 = (f32[3,8]{1,0:T(4,128)S(1)}, f32[3,8]{1,0:T(4,128)}, u32[]{:S(2)}) copy-start(f32[3,8]{1,0:T(4,128)} %param.25) | copy-start | bytes 292
  98.8 159.9 %copy-start.1 = (bf16[858,256]{1,0:T(8,128)(2,1)S(1)}, bf16[858,256]{1,0:T(8,128)(2,1)}, u32[]{:S(2)}) copy-start(bf16[858,256]{1,0:T(8,128)(2,1)} %param.19) | copy-start | bytes 1317892
  227.3 55.5 %reduce-scatter.13.cloned.1.call-start = ((), (), s32[]{:S(2)}) async-start(), calls=%async_computation.8 | async-start | bytes 163840
  258.7 44.8 %reduce-scatter.15.cloned.1.call-start = ((), (), s32[]{:S(2)}) async-start(), calls=%async_computation.9 | async-start | bytes 40960
  427.6 6.1 %copy-start.2 = (bf16[286,256]{1,0:T(8,128)(2,1)S(1)}, bf16[286,256]{1,0:T(8,128)(2,1)}, u32[]{:S(2)}) copy-start(bf16[286,256]{1,0:T(8,128)(2,1)} %param.20) | copy-start | bytes 439300
  427.6 6.6 %copy-start.4 = (bf16[858,256]{1,0:T(8,128)(2,1)S(1)}, bf16[858,256]{1,0:T(8,128)(2,1)}, u32[]{:S(2)}) copy-start(bf16[858,256]{1,0:T(8,128)(2,1)} %get-tuple-element.376) | copy-start | bytes 1317892
  427.7 6.6 %copy-start.8 = (s32[256,1]{0,1:T(1,128)S(1)}, s32[256,1]{0,1:T(1,128)}, u32[]{:S(2)}) copy-start(s32[256,1]{0,1:T(1,128)} %multiply_add_fusion.1) | copy-start | bytes 3076
Sparse Core Ops, SparseCore 0:
  18.8 17.3 reduce-scatter.8
  227.4 29.5 reduce-scatter.10
  259.4 20.4 reduce-scatter.12
  282.9 20.5 reduce-scatter.14
where the time goes:
time: 485 us; the launch traced here: 483 us
  other arithmetic  136 us (28%)
  blocking collectives  112 us (23%)
  matrix products  90.5 us (19%)
  local copies, waits for them, and re-layouts  69.5 us (14%)
  waiting for transfers between devices  41.9 us (9%)
  between operations  13.5 us (3%)
  starting transfers between devices  12.4 us (3%)
  loops' own time  7.74 us (2%)
    add x27, other arithmetic, count_slot(): running + (image_iota[:, None] == combined[slot_index][None, :]).astype(j...  128 us
    all_gather x8, blocking collectives, stacked_from(): blocks = lax.all_gather(blocks, axes[k], axis=0, tiled=True)  80 us
    dot_general x189, matrix products, add_far(): jnp.dot(source_hot, target_hot, precision=lax.Precision.HIGHEST)  62.6 us
    gather x3, local copies, waits for them, and re-layouts, local(): jnp.take_along_axis(normal_speed, kind_index, axis=0)  38.4 us
    reduce_scatter x2, waiting for transfers between devices, sum_by_axis(): nearer = lax.psum_scatter(array, axes[0], scatter_dimension=dim, tiled=True)  28.3 us
    all_to_all x1, blocking collectives, local(): lax.all_to_all(blocked, SEG, split_axis=2, concat_axis=2, tiled=True)  25.2 us
    unnamed x6, waiting for transfers between devices  13.6 us
    dot_general x1, matrix products, local(): jnp.dot(flat_ops, window, preferred_element_type=jnp.float32)  12.3 us
  transfers between devices with their start and end apart: 8, of which 2 were waited for; matrix products, arithmetic and copies ran while one was open for 59% of the time, Pallas kernels for 0%

commit v1 on v0

v1 whole, which is shorter than its diff:
```python
import functools

import jax
import jax.numpy as jnp
from jax import lax
from jax.experimental import pallas as pl
from jax.experimental.pallas import tpu as pltpu
from jax.sharding import PartitionSpec as P

NCOEF = 286
COEF = 858
MULT = 168
NTYPES = 8
NEAR_K = 27
FTYPES = 16
FAR_K = 189
LEAF = 256
HALO = 128
OCT_DEV = 8
OCTANTS = 1024
CAP = 4
SEG = 64
DEV = 128
KPAD = 896
OBLK = 32
NBLK = 27
HALF = 576
MSG = 640
GRP_SEG = ("grp", "seg")
LOGICAL = pl.DeviceIdType.LOGICAL
BF = jnp.bfloat16
F32 = jnp.float32
I32 = jnp.int32
VMEM = pltpu.VMEM


def dot(a, b, ca=1, cb=0):
    return lax.dot_general(a, b, (((ca,), (cb,)), ((), ())), preferred_element_type=F32)


def hot(mask):
    return jnp.where(mask, 1.0, 0.0).astype(BF)


def iota(shape, dim):
    return lax.broadcasted_iota(I32, shape, dim)


def remote(src, dst, send_sem, recv_sem, device):
    return pltpu.make_async_remote_copy(
        src_ref=src,
        dst_ref=dst,
        send_sem=send_sem,
        recv_sem=recv_sem,
        device_id=device,
        device_id_type=LOGICAL,
    )


def step_kernel(
    coeffs,
    tracer,
    up_op,
    far_ops,
    down_op,
    near_ops,
    face_dirs,
    leaf_octant,
    far_src,
    far_type,
    near_list,
    near_type,
    new_owner,
    arrived,
    raw_ops,
    ops,
    counts,
    group,
    mixed,
    halo_coeffs,
    halo_tracer,
    poles,
    far_count,
    local_own,
    local_in,
    local_edge,
    place,
    velocity,
    outgoing,
    slots,
    load_sem,
    halo_send,
    halo_recv,
    pole_send,
    pole_recv,
    pair_send,
    pair_recv,
    local_send,
    local_recv,
    move_send,
    move_recv,
):
    grp = lax.axis_index("grp")
    seg = lax.axis_index("seg")
    me = grp * SEG + seg
    partner = (1 - grp) * SEG + seg

    barrier = pltpu.get_barrier_semaphore()

    def greet(j, carry):
        pl.semaphore_signal(
            barrier, inc=1, device_id=lax.rem(me + j, DEV), device_id_type=LOGICAL
        )
        return carry

    lax.fori_loop(1, DEV, greet, 0)
    rows = COEF * NTYPES
    load = pltpu.make_async_copy(near_ops, raw_ops.at[pl.ds(0, rows)], load_sem)
    load.start()

    leaf_pole = dot(up_op[...], coeffs[...]).astype(BF)
    piece = hot(iota((16, LEAF), 0) == leaf_octant[...] - me * OCT_DEV)
    poles[pl.ds(me, 1)] = jnp.zeros((1, 16, 256), BF)
    poles[pl.ds(me, 1), :, 0:MULT] = dot(piece, leaf_pole, 1, 1).astype(BF)[None]
    pl.semaphore_wait(barrier, DEV - 1)

    def send_pole(j, carry):
        there = grp * SEG + lax.rem(seg + j, SEG)
        remote(poles.at[me], poles.at[me], pole_send, pole_recv, there).start()
        return carry

    lax.fori_loop(1, SEG, send_pole, 0)
    right = grp * SEG + lax.rem(seg + 1, SEG)
    left = grp * SEG + lax.rem(seg + SEG - 1, SEG)
    low = pl.ds(0, HALO)
    high = pl.ds(HALO, HALO)
    halos = [
        remote(coeffs.at[:, high], halo_coeffs.at[:, low], halo_send.at[0], halo_recv.at[0], right),
        remote(coeffs.at[:, low], halo_coeffs.at[:, high], halo_send.at[1], halo_recv.at[1], left),
        remote(tracer.at[:, high], halo_tracer.at[:, low], halo_send.at[2], halo_recv.at[2], right),
        remote(tracer.at[:, low], halo_tracer.at[:, high], halo_send.at[3], halo_recv.at[3], left),
    ]
    for copy in halos:
        copy.start()

    listed = near_list[...]
    inside = (listed >= HALO) & (listed < HALO + LEAF)
    spot = jnp.where(inside, listed - HALO, jnp.where(listed < HALO, listed + LEAF, listed))
    kind = near_type[...]
    one = jnp.ones_like(kind)
    first_word = jnp.where(kind < 4, one << (8 * jnp.minimum(kind, 3)), 0)
    other_word = jnp.where(
        (kind >= 4) & (kind < NTYPES), one << (8 * (jnp.clip(kind, 4, 7) - 4)), 0
    )
    slots[0] = spot
    slots[1] = first_word
    slots[2] = other_word

    def count_rows(block, carry):
        base = pl.multiple_of(block * 32, 32)
        place_of = iota((32, LEAF), 0) + base
        first = jnp.zeros((32, LEAF), I32)
        other = jnp.zeros((32, LEAF), I32)
        for k in range(NEAR_K):
            here = place_of == slots[0, k : k + 1, :]
            first = first + jnp.where(here, slots[1, k : k + 1, :], 0)
            other = other + jnp.where(here, slots[2, k : k + 1, :], 0)
        for t in range(NTYPES):
            word = first if t < 4 else other
            value = lax.shift_right_logical(word, jnp.full_like(word, 8 * (t % 4))) & 255
            counts[t, pl.ds(base, 32), :] = value.astype(F32).astype(BF)
        return carry

    lax.fori_loop(0, 16, count_rows, 0)

    for c in range(OCT_DEV):
        source = hot(iota((FAR_K, OCTANTS), 1) == far_src[:, c : c + 1])
        kind_hot = hot(iota((FAR_K, FTYPES), 1) == far_type[:, c : c + 1])
        far_count[c * FTYPES : (c + 1) * FTYPES, :] = dot(kind_hot, source, 0, 0).astype(BF)

    owner = new_owner[...].astype(F32)
    leaf_row = iota((LEAF, LEAF), 0)
    leaf_col = iota((LEAF, LEAF), 1)
    owner_row = jnp.sum(jnp.where(leaf_row == leaf_col, owner, 0.0), axis=0, keepdims=True)
    before = (leaf_row < leaf_col) & (owner == owner_row)
    rank = jnp.sum(jnp.where(before, 1.0, 0.0), axis=0, keepdims=True)
    target = (owner_row * 8.0 + rank).astype(I32)

    def place_rows(block, carry):
        base = pl.multiple_of(block * 256, 256)
        row = iota((256, LEAF), 0) + base
        place[0, pl.ds(base, 256), :] = hot(row == target)
        place[1, pl.ds(base, 256), :] = hot(row == target + CAP)
        return carry

    lax.fori_loop(0, 4, place_rows, 0)

    raw_ops[rows : NBLK * 256, :] = jnp.zeros((NBLK * 256 - rows, COEF), BF)
    for t in range(NTYPES):
        ops[:, t * KPAD + 768 : (t + 1) * KPAD] = jnp.zeros((NBLK * OBLK, 128), BF)
        group[t * KPAD + 848 : (t + 1) * KPAD, :] = jnp.zeros((48, LEAF), BF)
    turn_row = iota((256, 256), 0)
    turn = hot(iota((256, 256), 1) == lax.rem(turn_row, OBLK) * NTYPES + turn_row // OBLK)
    load.wait()

    def turn_block(b, carry):
        block = raw_ops[pl.ds(pl.multiple_of(b * 256, 256), 256), :]
        turned = dot(turn, block).astype(BF)
        out_rows = pl.ds(pl.multiple_of(b * OBLK, OBLK), OBLK)
        for t in range(NTYPES):
            ops[out_rows, t * KPAD : t * KPAD + COEF] = turned[t * OBLK : (t + 1) * OBLK, :]
        return carry

    lax.fori_loop(0, NBLK, turn_block, 0)

    remote(
        poles.at[pl.ds(0, SEG - 1)], poles.at[pl.ds(0, SEG - 1)], pole_send, pole_recv, partner
    ).wait_recv()
    mine = poles.at[pl.ds(grp * SEG, SEG)]
    pair = remote(mine, mine, pair_send, pair_recv, partner)
    pair.start()

    for copy in halos:
        copy.wait_recv()

    def gather_kind(t, carry):
        own = counts[t, 0:LEAF, :]
        edge = counts[t, LEAF : 2 * LEAF, :]
        base = pl.multiple_of(t * KPAD, KPAD)
        total = dot(coeffs[...], own) + dot(halo_coeffs[...], edge)
        group[pl.ds(base, COEF), :] = total.astype(BF)
        mixed[t] = dot(tracer[...], own) + dot(halo_tracer[...], edge)
        return carry

    lax.fori_loop(0, NTYPES, gather_kind, 0)

    pair.wait_recv()
    every = poles[...].astype(F32)
    edge_pole = every[:, 8:9, :]
    moved_edge = jnp.concatenate([jnp.zeros((1, 1, 256), F32), edge_pole[: DEV - 1]], axis=0)
    octant_pole = every[:, 0:8, :] + jnp.where(iota((DEV, 8, 256), 1) == 0, moved_edge, 0.0)
    octant_pole = octant_pole.reshape(OCTANTS, 256).astype(BF)
    grouped = dot(far_count[...], octant_pole).astype(BF)[:, 0:MULT]
    shifted = dot(far_ops[...], grouped, 1, 1).reshape(MULT, FTYPES, 128)
    same = lax.rem(iota((1, FTYPES, 128), 2), FTYPES) == iota((1, FTYPES, 128), 1)
    by_kind = jnp.sum(jnp.where(same, shifted, 0.0), axis=1).astype(BF)
    fold = hot(iota((16, 128), 1) // FTYPES == iota((16, 128), 0))
    local_own[...] = jnp.zeros((16, 256), BF)
    local_own[:, 0:MULT] = dot(fold, by_kind, 1, 1).astype(BF)
    holder = jnp.where(lax.rem(me, 2) == 0, me + 1, lax.rem(me + SEG + 1, DEV))
    to_holder = remote(local_own, local_in, local_send.at[0], local_recv.at[0], holder)
    to_holder.start()
    to_pair = remote(local_own, local_edge, local_send.at[1], local_recv.at[1], partner)
    to_pair.start()

    def near_rows(block, carry):
        here = pl.ds(pl.multiple_of(block * 288, 32), 288)
        velocity[here, :] = dot(ops[here, :], group[...])
        return carry

    lax.fori_loop(0, 3, near_rows, 0)

    to_holder.wait_recv()
    to_pair.wait_recv()
    row = iota((16, 256), 0)
    from_own = local_own[...].astype(F32)[0:1, :]
    from_pair = local_edge[...].astype(F32)[0:1, :]
    even = lax.rem(jnp.full((1, 256), me, I32), 2) == 0
    ninth = jnp.where(even, from_own, from_pair)
    nine = jnp.where(row < 8, local_in[...].astype(F32), jnp.where(row == 8, ninth, 0.0))
    leaf_local = dot(nine.astype(BF)[:, 0:MULT], piece, 0, 0).astype(BF)
    speed = velocity[0:COEF, :] + dot(down_op[...], leaf_local)

    flows = []
    total_in = jnp.zeros((1, LEAF), F32)
    for t in range(NTYPES):
        normal = (
            face_dirs[0, t] * speed[0:1, :]
            + face_dirs[1, t] * speed[NCOEF : NCOEF + 1, :]
            + face_dirs[2, t] * speed[2 * NCOEF : 2 * NCOEF + 1, :]
        )
        number = jnp.sum(jnp.where(kind == t, 1.0, 0.0), axis=0, keepdims=True)
        flow = jnp.maximum(normal, 0.0)
        flows.append((flow, number))
        total_in = total_in + flow * number
    denominator = 1.0 + total_in
    kept = jnp.ones((1, LEAF), F32)
    blended = jnp.zeros((NCOEF, LEAF), F32)
    for t, (flow, number) in enumerate(flows):
        weight = flow / denominator
        kept = kept - weight * number
        blended = blended + mixed[t] * weight
    blended = blended + tracer[...].astype(F32) * kept

    upper = speed[0:HALF, :].astype(BF)
    lower = jnp.concatenate(
        [speed[HALF:COEF, :], blended, jnp.zeros((8, LEAF), F32)], axis=0
    ).astype(BF)

    def pack_rows(block, carry):
        base = pl.ds(pl.multiple_of(block * 256, 256), 256)
        message = dot(place[0, base, :], upper, 1, 1) + dot(place[1, base, :], lower, 1, 1)
        message = jnp.concatenate([message, jnp.zeros((256, MSG - HALF), F32)], axis=1)
        outgoing[pl.ds(block * 32, 32)] = message.reshape(32, 8, MSG).astype(BF)
        return carry

    lax.fori_loop(0, 4, pack_rows, 0)

    def send_rows(j, carry):
        there = lax.rem(me + j, DEV)
        remote(outgoing.at[there], arrived.at[me], move_send, move_recv, there).start()
        return carry

    lax.fori_loop(1, DEV, send_rows, 0)
    arrived[pl.ds(me, 1)] = outgoing[pl.ds(me, 1)]

    for copy in halos:
        copy.wait_send()
    many = pl.ds(0, SEG - 1)
    remote(poles.at[many], poles.at[many], pole_send, pole_recv, partner).wait_send()
    pair.wait_send()
    to_holder.wait_send()
    to_pair.wait_send()
    most = pl.ds(0, DEV - 1)
    last = remote(outgoing.at[most], arrived.at[most], move_send, move_recv, partner)
    last.wait_send()
    last.wait_recv()


def step(*args):
    (
        coeffs,
        tracer,
        up_op,
        far_ops,
        down_op,
        near_ops,
        face_dirs,
        leaf_octant,
        far_src,
        far_type,
        near_list,
        near_type,
        new_owner,
    ) = args
    whole = pl.BlockSpec(memory_space=VMEM)
    dma = pltpu.SemaphoreType.DMA
    return pl.pallas_call(
        step_kernel,
        name="step",
        out_shape=jax.ShapeDtypeStruct((DEV, 8, MSG), BF),
        in_specs=[whole] * 5
        + [pl.BlockSpec(memory_space=pl.ANY), pl.BlockSpec(memory_space=pltpu.SMEM)]
        + [whole] * 6,
        out_specs=whole,
        scratch_shapes=[
            VMEM((NBLK * 256, COEF), BF),
            VMEM((NBLK * OBLK, NTYPES * KPAD), BF),
            VMEM((NTYPES, 2 * LEAF, LEAF), BF),
            VMEM((NTYPES * KPAD, LEAF), BF),
            VMEM((NTYPES, NCOEF, LEAF), F32),
            VMEM((COEF, LEAF), BF),
            VMEM((NCOEF, LEAF), BF),
            VMEM((DEV, 16, 256), BF),
            VMEM((128, OCTANTS), BF),
            VMEM((16, 256), BF),
            VMEM((16, 256), BF),
            VMEM((16, 256), BF),
            VMEM((2, 1024, LEAF), BF),
            VMEM((NBLK * OBLK, LEAF), F32),
            VMEM((DEV, 8, MSG), BF),
            VMEM((3, NEAR_K, LEAF), I32),
            dma,
            dma((4,)),
            dma((4,)),
            dma,
            dma,
            dma,
            dma,
            dma((2,)),
            dma((2,)),
            dma,
            dma,
        ],
        compiler_params=pltpu.CompilerParams(
            collective_id=0, has_side_effects=True, vmem_limit_bytes=64_000_000
        ),
    )(
        coeffs,
        tracer,
        up_op,
        far_ops.reshape(MULT * FTYPES, MULT),
        down_op,
        near_ops.reshape(COEF * NTYPES, COEF),
        face_dirs,
        leaf_octant.reshape(1, LEAF),
        far_src,
        far_type,
        near_list,
        near_type,
        new_owner,
    )


def turn_kernel(arrived, moved):
    block = arrived[...].astype(F32).reshape(256, MSG).astype(BF)
    row = iota((256, 256), 0)
    col = iota((256, 256), 1)
    wanted = (row // 8) * CAP + lax.rem(row, CAP) + 128 * (lax.rem(row, 8) // CAP)
    turned = dot(block, hot(col == wanted), 0, 0).astype(BF)
    moved[0:HALF, :] = turned[0:HALF, 0:128]
    moved[HALF : COEF + NCOEF, :] = turned[0 : COEF + NCOEF - HALF, 128:256]


def turned_rows(arrived):
    return pl.pallas_call(
        turn_kernel,
        name="turn",
        grid=(4,),
        out_shape=jax.ShapeDtypeStruct((COEF + NCOEF, DEV * CAP), BF),
        in_specs=[pl.BlockSpec((32, 8, MSG), lambda g: (g, 0, 0))],
        out_specs=pl.BlockSpec((COEF + NCOEF, 128), lambda g: (0, g)),
        compiler_params=pltpu.CompilerParams(dimension_semantics=("arbitrary",)),
    )(arrived)


def local(*args):
    return turned_rows(step(*args))


def solution(mesh):
    split = P(None, GRP_SEG)
    in_specs = (
        split,
        split,
        P(),
        P(),
        P(),
        P(),
        P(),
        P(GRP_SEG),
        split,
        split,
        split,
        split,
        P(GRP_SEG, None),
    )
    return jax.shard_map(local, mesh=mesh, in_specs=in_specs, out_specs=split, check_vma=False)
```

time: 485 us -> 68.9 us (0.14)
  other arithmetic: 136 us -> 0 us
  blocking collectives: 112 us -> 0 us
  matrix products: 90.5 us -> 0 us
  local copies, waits for them, and re-layouts: 69.5 us -> 6.28 us
  Pallas kernels: 0 us -> 61.9 us
  waiting for transfers between devices: 41.9 us -> 0 us
  between operations: 13.5 us -> 0.01 us
  starting transfers between devices: 12.4 us -> 0 us
  loops' own time: 7.74 us -> 0 us
    add x59 -> x0, other arithmetic: 134 us -> none  [the longest x27 128 us: count_slot(): running + (image_iota[:, None] == combined[slot_index][None, :]).astype(j...]
    dot_general x197 -> x0, matrix products: 90.5 us -> none  [the longest x189 62.6 us: add_far(): jnp.dot(source_hot, target_hot, precision=lax.Precision.HIGHEST)]
    all_gather x8 -> x0, blocking collectives: 80 us -> none  [stacked_from(): blocks = lax.all_gather(blocks, axes[k], axis=0, tiled=True)]
    pallas_call x0 -> x2, Pallas kernels: none -> 61.9 us  [the longest x1 57.9 us: step(): pl.pallas_call(step_kernel, name='step', out_shape=jax.ShapeDtypeStruct((...]
    gather x3 -> x0, local copies, waits for them, and re-layouts: 38.4 us -> none  [local(): jnp.take_along_axis(normal_speed, kind_index, axis=0)]
    all_to_all x2 -> x0, blocking collectives: 32.3 us -> none  [the longest x1 25.2 us: local(): lax.all_to_all(blocked, SEG, split_axis=2, concat_axis=2, tiled=True)]
    reduce_scatter x2 -> x0, waiting for transfers between devices: 28.3 us -> none  [sum_by_axis(): nearer = lax.psum_scatter(array, axes[0], scatter_dimension=dim, tiled=True)]
    reshape x7 -> x0, local copies, waits for them, and re-layouts: 18.5 us -> none  [the longest x1 11.7 us: local(): images = images.reshape(coef_rows, near_kinds * window_span)]
  transfers between devices with their start and end apart: 8 -> 0, of which waited for: 2 -> 0; matrix products, arithmetic and copies ran while one was open for 59% -> 0% of each run, Pallas kernels for 0% -> 0%
where the time goes in v1:
time: 68.9 us; the launch traced here: 68.2 us
  Pallas kernels  61.9 us (90%)
  local copies, waits for them, and re-layouts  6.28 us (9%)
    pallas_call x1, Pallas kernels, step(): pl.pallas_call(step_kernel, name='step', out_shape=jax.ShapeDtypeStruct((...  57.9 us
    unnamed x4, local copies, waits for them, and re-layouts  6.28 us
    pallas_call x1, Pallas kernels, turned_rows(): pl.pallas_call(turn_kernel, name='turn', grid=(4,), out_shape=jax.ShapeDt...  4 us

profile of v1, /device:TPU:1, one launch (start us, length us, event | category | flops | bytes accessed | tf_op | source)
XLA Modules:
  0.0 68.2 jit_solution(5796735728422215800)
XLA Ops:
  0.0 1.4 %copy.15.far_src = s32[189,8]{1,0:T(8,128)} copy(s32[189,8]{0,1:T(8,128)} %param.21) | data formatting | bytes 12096 | tf_op args[8]
  1.4 1.5 %copy.16.far_type = s32[189,8]{1,0:T(8,128)} copy(s32[189,8]{0,1:T(8,128)} %param.22) | data formatting | bytes 12096 | tf_op args[9]
  2.9 1.5 %copy.17.new_owner = s32[256,1]{1,0:T(8,128)} copy(s32[256,1]{0,1:T(1,128)} %param.25) | data formatting | bytes 2048 | tf_op args[12]
  4.4 1.9 %copy.14.down_op = bf16[858,168]{1,0:T(8,128)(2,1)} copy(bf16[858,168]{0,1:T(8,128)(2,1)} %param.17) | data formatting | bytes 576576 | tf_op args[4]
  6.3 57.9 %step.1.arrived = bf16[128,8,640]{2,1,0:T(8,128)(2,1)} custom-call(bf16[858,256]{1,0:T(8,128)(2,1)} %coeffs.1, bf16[286,256]{1,0:T(8,128)(2,1)} %tracer.1, bf16[168,858]{1,0:T(8,128)(2,1)} %up_op.1, bf16[2688,168]{1,0:T(8,128)(2,1)} %bitcast.4, bf16[858,168]{1,0:T(8,128)(2,1)} %copy.14.down_op, bf16[6864,858]{1,0:T(8,128)(2,1)} %bitcast.3, ...), custom_call_target="tpu_custom_call" | custom-call | tf_op jit(solution)/shard_map/step/pallas_call | solution.py:348
  64.2 4.0 %turn.1 = bf16[1144,512]{1,0:T(8,128)(2,1)} custom-call(bf16[128,8,640]{2,1,0:T(8,128)(2,1)} %step.1.arrived), custom_call_target="tpu_custom_call" | custom-call | tf_op jit(solution)/shard_map/turn/pallas_call | solution.py:416

commit v2 on v1

v2 whole, which is shorter than its diff:
```python
import functools

import jax
import jax.numpy as jnp
from jax import lax
from jax.experimental import pallas as pl
from jax.experimental.pallas import tpu as pltpu
from jax.sharding import PartitionSpec as P

NCOEF = 286
COEF = 858
MULT = 168
NTYPES = 8
NEAR_K = 27
FTYPES = 16
FAR_K = 189
LEAF = 256
HALO = 128
OCT_DEV = 8
OCTANTS = 1024
CAP = 4
SEG = 64
DEV = 128
KPAD = 896
OBLK = 32
NBLK = 27
FRONT = 640
BACK = 512
REST = 504
GRP_SEG = ("grp", "seg")
LOGICAL = pl.DeviceIdType.LOGICAL
BF = jnp.bfloat16
F32 = jnp.float32
I32 = jnp.int32
VMEM = pltpu.VMEM


def dot(a, b, ca=1, cb=0):
    return lax.dot_general(a, b, (((ca,), (cb,)), ((), ())), preferred_element_type=F32)


def hot(mask):
    return jnp.where(mask, 1.0, 0.0).astype(BF)


def iota(shape, dim):
    return lax.broadcasted_iota(I32, shape, dim)


def remote(src, dst, send_sem, recv_sem, device):
    return pltpu.make_async_remote_copy(
        src_ref=src,
        dst_ref=dst,
        send_sem=send_sem,
        recv_sem=recv_sem,
        device_id=device,
        device_id_type=LOGICAL,
    )


def step_kernel(
    coeffs_hbm,
    tracer_hbm,
    up_hbm,
    far_hbm,
    down_hbm,
    near_hbm,
    face_dirs,
    octant_hbm,
    source_hbm,
    type_hbm,
    list_hbm,
    kind_hbm,
    owner_hbm,
    arrived_front,
    arrived_back,
    window,
    tracers,
    up_op,
    far_ops,
    down_op,
    leaf_octant,
    far_src,
    far_type,
    near_list,
    near_type,
    new_owner,
    raw_ops,
    ops,
    counts,
    group,
    mixed,
    poles,
    far_count,
    local_own,
    local_in,
    local_edge,
    place,
    velocity,
    front,
    back,
    slots,
    load_sem,
    halo_send,
    halo_recv,
    pole_send,
    pole_recv,
    pair_send,
    pair_recv,
    local_send,
    local_recv,
    move_send,
    move_recv,
):
    grp = lax.axis_index("grp")
    seg = lax.axis_index("seg")
    me = grp * SEG + seg
    partner = (1 - grp) * SEG + seg
    own_lanes = pl.ds(0, LEAF)
    rows = COEF * NTYPES

    def load(source, target, k):
        copy = pltpu.make_async_copy(source, target, load_sem.at[k])
        copy.start()
        return copy

    loads = [
        load(coeffs_hbm, window.at[:, own_lanes], 0),
        load(up_hbm, up_op, 1),
        load(octant_hbm, leaf_octant, 2),
        load(list_hbm, near_list, 3),
        load(kind_hbm, near_type, 4),
        load(source_hbm, far_src, 5),
        load(type_hbm, far_type, 6),
        load(owner_hbm, new_owner, 7),
        load(tracer_hbm, tracers.at[:, own_lanes], 8),
        load(near_hbm, raw_ops.at[pl.ds(0, rows)], 9),
        load(far_hbm, far_ops, 10),
        load(down_hbm, down_op, 11),
    ]

    barrier = pltpu.get_barrier_semaphore()

    def greet(j, carry):
        there = grp * SEG + lax.rem(seg + j, SEG)
        pl.semaphore_signal(barrier, inc=1, device_id=there, device_id_type=LOGICAL)
        return carry

    lax.fori_loop(1, SEG, greet, 0)
    pl.semaphore_signal(barrier, inc=1, device_id=partner, device_id_type=LOGICAL)

    for copy in loads[0:3]:
        copy.wait()
    leaf_pole = dot(up_op[...], window[:, 0:LEAF]).astype(BF)
    piece = hot(iota((16, LEAF), 0) == leaf_octant[...] - me * OCT_DEV)
    poles[pl.ds(me, 1)] = jnp.zeros((1, 16, 256), BF)
    poles[pl.ds(me, 1), :, 0:MULT] = dot(piece, leaf_pole, 1, 1).astype(BF)[None]

    for copy in loads[3:9]:
        copy.wait()
    listed = near_list[...]
    inside = (listed >= HALO) & (listed < HALO + LEAF)
    spot = jnp.where(inside, listed - HALO, jnp.where(listed < HALO, listed + LEAF, listed))
    kind = near_type[...]
    one = jnp.ones_like(kind)
    first_word = jnp.where(kind < 4, one << (8 * jnp.minimum(kind, 3)), 0)
    other_word = jnp.where(
        (kind >= 4) & (kind < NTYPES), one << (8 * (jnp.clip(kind, 4, 7) - 4)), 0
    )
    slots[0] = spot
    slots[1] = first_word
    slots[2] = other_word

    def count_rows(block, carry):
        base = pl.multiple_of(block * 32, 32)
        place_of = iota((32, LEAF), 0) + base
        first = jnp.zeros((32, LEAF), I32)
        other = jnp.zeros((32, LEAF), I32)
        for k in range(NEAR_K):
            here = place_of == slots[0, k : k + 1, :]
            first = first + jnp.where(here, slots[1, k : k + 1, :], 0)
            other = other + jnp.where(here, slots[2, k : k + 1, :], 0)
        for t in range(NTYPES):
            word = first if t < 4 else other
            value = lax.shift_right_logical(word, jnp.full_like(word, 8 * (t % 4))) & 255
            counts[t, pl.ds(base, 32), :] = value.astype(F32).astype(BF)
        return carry

    lax.fori_loop(0, 16, count_rows, 0)

    pl.semaphore_wait(barrier, SEG)

    def send_pole(j, carry):
        there = grp * SEG + lax.rem(seg + j, SEG)
        remote(poles.at[me], poles.at[me], pole_send, pole_recv, there).start()
        return carry

    right = grp * SEG + lax.rem(seg + 1, SEG)
    left = grp * SEG + lax.rem(seg + SEG - 1, SEG)
    low = pl.ds(0, HALO)
    high = pl.ds(HALO, HALO)
    to_low = pl.ds(LEAF, HALO)
    to_high = pl.ds(LEAF + HALO, HALO)
    halos = [
        remote(src.at[:, lanes], src.at[:, there], halo_send.at[k], halo_recv.at[k], device)
        for k, (src, lanes, there, device) in enumerate(
            (
                (window, high, to_low, right),
                (window, low, to_high, left),
                (tracers, high, to_low, right),
                (tracers, low, to_high, left),
            )
        )
    ]
    lax.fori_loop(1, SEG, send_pole, 0)
    for copy in halos:
        copy.start()

    for c in range(OCT_DEV):
        source = hot(iota((OCTANTS, FAR_K), 0) == far_src[c : c + 1, :])
        kind_hot = hot(iota((FTYPES, FAR_K), 0) == far_type[c : c + 1, :])
        far_count[c * FTYPES : (c + 1) * FTYPES, :] = dot(kind_hot, source, 1, 1).astype(BF)

    owner_row = new_owner[...].astype(F32)
    leaf_row = iota((LEAF, LEAF), 0)
    leaf_col = iota((LEAF, LEAF), 1)
    owner = jnp.sum(jnp.where(leaf_row == leaf_col, owner_row, 0.0), axis=1, keepdims=True)
    before = (leaf_row < leaf_col) & (owner == owner_row)
    rank = jnp.sum(jnp.where(before, 1.0, 0.0), axis=0, keepdims=True)
    target = (owner_row * float(CAP) + rank).astype(I32)
    place[...] = hot(iota((DEV * CAP, LEAF), 0) == target)

    raw_ops[rows : NBLK * 256, :] = jnp.zeros((NBLK * 256 - rows, COEF), BF)
    for t in range(NTYPES):
        ops[:, t * KPAD + 768 : (t + 1) * KPAD] = jnp.zeros((NBLK * OBLK, 128), BF)
        group[t * KPAD + 848 : (t + 1) * KPAD, :] = jnp.zeros((48, LEAF), BF)
    turn_row = iota((256, 256), 0)
    turn = hot(iota((256, 256), 1) == lax.rem(turn_row, OBLK) * NTYPES + turn_row // OBLK)
    for copy in loads[9:12]:
        copy.wait()

    def turn_blocks(b, carry):
        for part in range(3):
            at = b * 3 + part
            block = raw_ops[pl.ds(pl.multiple_of(at * 256, 256), 256), :]
            turned = dot(turn, block).astype(BF)
            out_rows = pl.ds(pl.multiple_of(at * OBLK, OBLK), OBLK)
            for t in range(NTYPES):
                ops[out_rows, t * KPAD : t * KPAD + COEF] = turned[t * OBLK : (t + 1) * OBLK, :]
        return carry

    lax.fori_loop(0, 6, turn_blocks, 0)

    many = pl.ds(0, SEG - 1)
    all_poles = remote(poles.at[many], poles.at[many], pole_send, pole_recv, partner)
    all_poles.wait_recv()
    mine = poles.at[pl.ds(grp * SEG, SEG)]
    pair = remote(mine, mine, pair_send, pair_recv, partner)
    pair.start()
    lax.fori_loop(6, 9, turn_blocks, 0)

    for copy in halos:
        copy.wait_recv()

    def gather_kinds(pair_of, carry):
        for part in range(2):
            t = pair_of * 2 + part
            base = pl.multiple_of(t * KPAD, KPAD)
            group[pl.ds(base, COEF), :] = dot(window[...], counts[t]).astype(BF)
            mixed[t] = dot(tracers[...], counts[t])
        return carry

    lax.fori_loop(0, NTYPES // 2, gather_kinds, 0)

    pair.wait_recv()
    every = poles[...].astype(F32)
    edge_pole = every[:, 8:9, :]
    moved_edge = jnp.concatenate([jnp.zeros((1, 1, 256), F32), edge_pole[: DEV - 1]], axis=0)
    octant_pole = every[:, 0:8, :] + jnp.where(iota((DEV, 8, 256), 1) == 0, moved_edge, 0.0)
    octant_pole = octant_pole.reshape(OCTANTS, 256).astype(BF)
    grouped = dot(far_count[...], octant_pole).astype(BF)[:, 0:MULT]
    shifted = dot(far_ops[...], grouped, 1, 1).reshape(MULT, FTYPES, 128)
    same = lax.rem(iota((1, FTYPES, 128), 2), FTYPES) == iota((1, FTYPES, 128), 1)
    by_kind = jnp.sum(jnp.where(same, shifted, 0.0), axis=1).astype(BF)
    fold = hot(iota((16, 128), 1) // FTYPES == iota((16, 128), 0))
    local_own[...] = jnp.zeros((16, 256), BF)
    local_own[:, 0:MULT] = dot(fold, by_kind, 1, 1).astype(BF)
    holder = jnp.where(lax.rem(me, 2) == 0, me + 1, lax.rem(me + SEG + 1, DEV))
    to_holder = remote(local_own, local_in, local_send.at[0], local_recv.at[0], holder)
    to_holder.start()
    to_pair = remote(local_own, local_edge, local_send.at[1], local_recv.at[1], partner)
    to_pair.start()

    def near_rows(block, carry):
        here = pl.ds(pl.multiple_of(block * 320, 32), 320)
        velocity[here, :] = dot(ops[here, :], group[...])
        return carry

    lax.fori_loop(0, 2, near_rows, 0)

    to_holder.wait_recv()
    to_pair.wait_recv()
    row = iota((16, 256), 0)
    from_own = local_own[...].astype(F32)[0:1, :]
    from_pair = local_edge[...].astype(F32)[0:1, :]
    even = lax.rem(jnp.full((1, 256), me, I32), 2) == 0
    ninth = jnp.where(even, from_own, from_pair)
    nine = jnp.where(row < 8, local_in[...].astype(F32), jnp.where(row == 8, ninth, 0.0))
    leaf_local = dot(nine.astype(BF)[:, 0:MULT], piece, 0, 0).astype(BF)
    velocity[0:FRONT, :] = velocity[0:FRONT, :] + dot(down_op[:, 0:FRONT], leaf_local, 0, 0)

    message = dot(place[...], velocity[0:FRONT, :].astype(BF), 1, 1)
    front[...] = message.reshape(DEV, CAP, FRONT).astype(BF)

    def send_front(j, carry):
        there = lax.rem(me + j, DEV)
        remote(front.at[there], arrived_front.at[me], move_send.at[0], move_recv.at[0], there).start()
        return carry

    lax.fori_loop(1, DEV, send_front, 0)

    rest = dot(ops[FRONT : NBLK * OBLK, :], group[...])[0 : COEF - FRONT, :]
    rest = rest + dot(down_op[:, FRONT:COEF], leaf_local, 0, 0)

    flows = []
    total_in = jnp.zeros((1, LEAF), F32)
    for t in range(NTYPES):
        normal = (
            face_dirs[0, t] * velocity[0:1, :]
            + face_dirs[1, t] * velocity[NCOEF : NCOEF + 1, :]
            + face_dirs[2, t] * velocity[2 * NCOEF : 2 * NCOEF + 1, :]
        )
        number = jnp.sum(jnp.where(kind == t, 1.0, 0.0), axis=0, keepdims=True)
        flow = jnp.maximum(normal, 0.0)
        flows.append((flow, number))
        total_in = total_in + flow * number
    denominator = 1.0 + total_in
    kept = jnp.ones((1, LEAF), F32)
    blended = jnp.zeros((NCOEF, LEAF), F32)
    for t, (flow, number) in enumerate(flows):
        weight = flow / denominator
        kept = kept - weight * number
        blended = blended + mixed[t] * weight
    blended = blended + tracers[:, 0:LEAF].astype(F32) * kept

    lower = jnp.concatenate([rest, blended, jnp.zeros((BACK - REST, LEAF), F32)], axis=0)
    message = dot(place[...], lower.astype(BF), 1, 1)
    back[...] = message.reshape(DEV, CAP, BACK).astype(BF)

    def send_back(j, carry):
        there = lax.rem(me + j, DEV)
        remote(back.at[there], arrived_back.at[me], move_send.at[1], move_recv.at[1], there).start()
        return carry

    lax.fori_loop(1, DEV, send_back, 0)
    arrived_front[pl.ds(me, 1)] = front[pl.ds(me, 1)]
    arrived_back[pl.ds(me, 1)] = back[pl.ds(me, 1)]

    for copy in halos:
        copy.wait_send()
    all_poles.wait_send()
    pair.wait_send()
    to_holder.wait_send()
    to_pair.wait_send()
    most = pl.ds(0, DEV - 1)
    for k, (sent, got) in enumerate(((front, arrived_front), (back, arrived_back))):
        last = remote(sent.at[most], got.at[most], move_send.at[k], move_recv.at[k], partner)
        last.wait_send()
        last.wait_recv()


def step(*args):
    (
        coeffs,
        tracer,
        up_op,
        far_ops,
        down_op,
        near_ops,
        face_dirs,
        leaf_octant,
        far_src,
        far_type,
        near_list,
        near_type,
        new_owner,
    ) = args
    whole = pl.BlockSpec(memory_space=VMEM)
    anywhere = pl.BlockSpec(memory_space=pl.ANY)
    dma = pltpu.SemaphoreType.DMA
    return pl.pallas_call(
        step_kernel,
        name="step",
        out_shape=(
            jax.ShapeDtypeStruct((DEV, CAP, FRONT), BF),
            jax.ShapeDtypeStruct((DEV, CAP, BACK), BF),
        ),
        in_specs=[anywhere] * 6 + [pl.BlockSpec(memory_space=pltpu.SMEM)] + [anywhere] * 6,
        out_specs=(whole, whole),
        scratch_shapes=[
            VMEM((COEF, 2 * LEAF), BF),
            VMEM((NCOEF, 2 * LEAF), BF),
            VMEM((MULT, COEF), BF),
            VMEM((MULT * FTYPES, MULT), BF),
            VMEM((MULT, COEF), BF),
            VMEM((1, LEAF), I32),
            VMEM((OCT_DEV, FAR_K), I32),
            VMEM((OCT_DEV, FAR_K), I32),
            VMEM((NEAR_K, LEAF), I32),
            VMEM((NEAR_K, LEAF), I32),
            VMEM((1, LEAF), I32),
            VMEM((NBLK * 256, COEF), BF),
            VMEM((NBLK * OBLK, NTYPES * KPAD), BF),
            VMEM((NTYPES, 2 * LEAF, LEAF), BF),
            VMEM((NTYPES * KPAD, LEAF), BF),
            VMEM((NTYPES, NCOEF, LEAF), F32),
            VMEM((DEV, 16, 256), BF),
            VMEM((128, OCTANTS), BF),
            VMEM((16, 256), BF),
            VMEM((16, 256), BF),
            VMEM((16, 256), BF),
            VMEM((DEV * CAP, LEAF), BF),
            VMEM((FRONT, LEAF), F32),
            VMEM((DEV, CAP, FRONT), BF),
            VMEM((DEV, CAP, BACK), BF),
            VMEM((3, NEAR_K, LEAF), I32),
            dma((12,)),
            dma((4,)),
            dma((4,)),
            dma,
            dma,
            dma,
            dma,
            dma((2,)),
            dma((2,)),
            dma((2,)),
            dma((2,)),
        ],
        compiler_params=pltpu.CompilerParams(
            collective_id=0, has_side_effects=True, vmem_limit_bytes=67_043_328
        ),
    )(
        coeffs,
        tracer,
        up_op,
        far_ops.reshape(MULT * FTYPES, MULT),
        down_op.T,
        near_ops.reshape(COEF * NTYPES, COEF),
        face_dirs,
        leaf_octant.reshape(1, LEAF),
        far_src.T,
        far_type.T,
        near_list,
        near_type,
        new_owner.reshape(1, LEAF),
    )


def turn_kernel(front, back, moved):
    slots = DEV * CAP
    moved[0:FRONT, :] = front[...].astype(F32).reshape(slots, FRONT).T.astype(BF)
    turned = back[...].astype(F32).reshape(slots, BACK).T
    moved[FRONT : COEF + NCOEF, :] = turned[0:REST].astype(BF)


def local(*args):
    return pl.pallas_call(
        turn_kernel,
        name="turn",
        out_shape=jax.ShapeDtypeStruct((COEF + NCOEF, DEV * CAP), BF),
    )(*step(*args))


def solution(mesh):
    split = P(None, GRP_SEG)
    in_specs = (
        split,
        split,
        P(),
        P(),
        P(),
        P(),
        P(),
        P(GRP_SEG),
        split,
        split,
        split,
        split,
        P(GRP_SEG, None),
    )
    return jax.shard_map(local, mesh=mesh, in_specs=in_specs, out_specs=split, check_vma=False)
```

time: 68.9 us -> 55.6 us (0.81)
  Pallas kernels: 61.9 us -> 55.5 us
  local copies, waits for them, and re-layouts: 6.28 us -> 0 us
    pallas_call x2, Pallas kernels: 61.9 us -> 55.5 us  [the longest x1 52.8 us: step(): pl.pallas_call(step_kernel, name='step', out_shape=(jax.ShapeDtypeStruct(...]
    unnamed x4 -> x0, local copies, waits for them, and re-layouts: 6.28 us -> none
where the time goes in v2:
time: 55.6 us; the launch traced here: 55.5 us
  Pallas kernels  55.5 us (100%)
    pallas_call x1, Pallas kernels, step(): pl.pallas_call(step_kernel, name='step', out_shape=(jax.ShapeDtypeStruct(...  52.8 us
    pallas_call x1, Pallas kernels, local(): pl.pallas_call(turn_kernel, name='turn', out_shape=jax.ShapeDtypeStruct((...  2.66 us

profile of v2, /device:TPU:1, one launch (start us, length us, event | category | flops | bytes accessed | tf_op | source)
XLA Modules:
  0.0 55.5 jit_solution(11012632654584012606)
XLA Ops:
  0.0 52.8 %step.1 = (bf16[128,4,640]{2,1,0:T(4,128)(2,1)}, bf16[128,4,512]{2,1,0:T(4,128)(2,1)}) custom-call(bf16[858,256]{1,0:T(8,128)(2,1)} %coeffs_hbm.1, bf16[286,256]{1,0:T(8,128)(2,1)} %tracer_hbm.1, bf16[168,858]{1,0:T(8,128)(2,1)} %up_hbm.1, bf16[2688,168]{1,0:T(8,128)(2,1)} %bitcast.8, bf16[168,858]{1,0:T(8,128)(2,1)} %bitcast.9, bf16[6864,858]{1,0:T(8,128)(2,1)} %bitcast.7, ...), custom_call_target="tpu_custom_call" | custom-call | tf_op jit(solution)/shard_map/step/pallas_call | solution.py:391
  52.8 2.7 %turn.1 = bf16[1144,512]{1,0:T(8,128)(2,1)} custom-call(bf16[128,4,640]{2,1,0:T(4,128)(2,1)} %get-tuple-element.7.front, bf16[128,4,512]{2,1,0:T(4,128)(2,1)} %get-tuple-element.8.back), custom_call_target="tpu_custom_call" | custom-call | tf_op jit(solution)/shard_map/turn/pallas_call | solution.py:467

commit v3 on v2

--- a/solution.py
+++ b/solution.py
@@ -27,6 +27,14 @@
 FRONT = 640
 BACK = 512
 REST = 504
+LINE = 4
+PLANE = 16
+TARGETS = 144
+CUT = 88
+CHUNKS = 9
+CHUNK = 768
+CUT_BACK = 80
+GREETINGS = 22
 GRP_SEG = ("grp", "seg")
 LOGICAL = pl.DeviceIdType.LOGICAL
 BF = jnp.bfloat16
@@ -92,9 +100,10 @@
     mixed,
     poles,
     far_count,
-    local_own,
-    local_in,
-    local_edge,
+    source_in,
+    type_in,
+    source_edge,
+    type_edge,
     place,
     velocity,
     front,
@@ -103,12 +112,14 @@
     load_sem,
     halo_send,
     halo_recv,
-    pole_send,
-    pole_recv,
+    list_send,
+    list_recv,
+    line_send,
+    line_recv,
+    plane_send,
+    plane_recv,
     pair_send,
     pair_recv,
-    local_send,
-    local_recv,
     move_send,
     move_recv,
 ):
@@ -128,75 +139,74 @@
         load(coeffs_hbm, window.at[:, own_lanes], 0),
         load(up_hbm, up_op, 1),
         load(octant_hbm, leaf_octant, 2),
-        load(list_hbm, near_list, 3),
-        load(kind_hbm, near_type, 4),
-        load(source_hbm, far_src, 5),
-        load(type_hbm, far_type, 6),
-        load(owner_hbm, new_owner, 7),
-        load(tracer_hbm, tracers.at[:, own_lanes], 8),
-        load(near_hbm, raw_ops.at[pl.ds(0, rows)], 9),
-        load(far_hbm, far_ops, 10),
-        load(down_hbm, down_op, 11),
+        load(tracer_hbm, tracers.at[:, own_lanes], 3),
+        load(source_hbm, far_src, 4),
+        load(type_hbm, far_type, 5),
+        load(list_hbm, near_list, 6),
+        load(kind_hbm, near_type, 7),
+        load(owner_hbm, new_owner, 8),
+        load(far_hbm, far_ops, 9),
+        load(down_hbm, down_op, 10),
     ]
+    chunks = []
+    for k in range(CHUNKS):
+        start = k * CHUNK
+        part_of = pl.ds(start, min(CHUNK, rows - start))
+        chunks.append(load(near_hbm.at[part_of], raw_ops.at[part_of], 11 + k))
+
+    right = grp * SEG + lax.rem(seg + 1, SEG)
+    left = grp * SEG + lax.rem(seg + SEG - 1, SEG)
+    holder = jnp.where(lax.rem(me, 2) == 0, me + 1, lax.rem(me + SEG + 1, DEV))
+    lister = jnp.where(lax.rem(me, 2) == 0, lax.rem(me + SEG - 1, DEV), me - 1)
+
+    def on_line(j):
+        return grp * SEG + (seg // LINE) * LINE + lax.rem(seg + j, LINE)
+
+    def in_plane(j):
+        return grp * SEG + lax.rem(seg + LINE * j, SEG)
 
     barrier = pltpu.get_barrier_semaphore()
 
-    def greet(j, carry):
-        there = grp * SEG + lax.rem(seg + j, SEG)
+    def greet(there):
         pl.semaphore_signal(barrier, inc=1, device_id=there, device_id_type=LOGICAL)
-        return carry
-
-    lax.fori_loop(1, SEG, greet, 0)
-    pl.semaphore_signal(barrier, inc=1, device_id=partner, device_id_type=LOGICAL)
+
+    greet(right)
+    greet(left)
+    for j in range(1, LINE):
+        greet(on_line(j))
+    greet(partner)
+    greet(lister)
+
+    def greet_plane(j, carry):
+        greet(in_plane(j))
+        return carry
+
+    lax.fori_loop(1, PLANE, greet_plane, 0)
 
     for copy in loads[0:3]:
         copy.wait()
     leaf_pole = dot(up_op[...], window[:, 0:LEAF]).astype(BF)
     piece = hot(iota((16, LEAF), 0) == leaf_octant[...] - me * OCT_DEV)
-    poles[pl.ds(me, 1)] = jnp.zeros((1, 16, 256), BF)
-    poles[pl.ds(me, 1), :, 0:MULT] = dot(piece, leaf_pole, 1, 1).astype(BF)[None]
-
-    for copy in loads[3:9]:
+    part = dot(piece, leaf_pole, 1, 1)
+    ninth = part[8:9, :]
+    part_row = iota((8, MULT), 0)
+    lane_in = iota((MULT, 256), 0)
+    lane_out = iota((MULT, 256), 1)
+    spread = (
+        (part[0:8, :], lane_out == lane_in),
+        (jnp.where(part_row == 0, ninth, 0.0), (lane_out == lane_in + MULT) & (lane_in < CUT)),
+        (jnp.where(part_row == 1, ninth, 0.0), (lane_out == lane_in + CUT_BACK) & (lane_in >= CUT)),
+    )
+    packed = jnp.zeros((8, 256), F32)
+    for value, lanes in spread:
+        packed = packed + dot(value.astype(BF), hot(lanes))
+    poles[pl.ds(me, 1)] = packed.astype(BF)[None]
+
+    for copy in loads[3:6]:
         copy.wait()
-    listed = near_list[...]
-    inside = (listed >= HALO) & (listed < HALO + LEAF)
-    spot = jnp.where(inside, listed - HALO, jnp.where(listed < HALO, listed + LEAF, listed))
-    kind = near_type[...]
-    one = jnp.ones_like(kind)
-    first_word = jnp.where(kind < 4, one << (8 * jnp.minimum(kind, 3)), 0)
-    other_word = jnp.where(
-        (kind >= 4) & (kind < NTYPES), one << (8 * (jnp.clip(kind, 4, 7) - 4)), 0
-    )
-    slots[0] = spot
-    slots[1] = first_word
-    slots[2] = other_word
-
-    def count_rows(block, carry):
-        base = pl.multiple_of(block * 32, 32)
-        place_of = iota((32, LEAF), 0) + base
-        first = jnp.zeros((32, LEAF), I32)
-        other = jnp.zeros((32, LEAF), I32)
-        for k in range(NEAR_K):
-            here = place_of == slots[0, k : k + 1, :]
-            first = first + jnp.where(here, slots[1, k : k + 1, :], 0)
-            other = other + jnp.where(here, slots[2, k : k + 1, :], 0)
-        for t in range(NTYPES):
-            word = first if t < 4 else other
-            value = lax.shift_right_logical(word, jnp.full_like(word, 8 * (t % 4))) & 255
-            counts[t, pl.ds(base, 32), :] = value.astype(F32).astype(BF)
-        return carry
-
-    lax.fori_loop(0, 16, count_rows, 0)
-
-    pl.semaphore_wait(barrier, SEG)
-
-    def send_pole(j, carry):
-        there = grp * SEG + lax.rem(seg + j, SEG)
-        remote(poles.at[me], poles.at[me], pole_send, pole_recv, there).start()
-        return carry
-
-    right = grp * SEG + lax.rem(seg + 1, SEG)
-    left = grp * SEG + lax.rem(seg + SEG - 1, SEG)
+    pl.semaphore_wait(barrier, GREETINGS)
+    for j in range(1, LINE):
+        remote(poles.at[me], poles.at[me], line_send, line_recv, on_line(j)).start()
     low = pl.ds(0, HALO)
     high = pl.ds(HALO, HALO)
     to_low = pl.ds(LEAF, HALO)
@@ -212,14 +222,64 @@
             )
         )
     ]
-    lax.fori_loop(1, SEG, send_pole, 0)
-    for copy in halos:
+    lists = [
+        remote(src, there, list_send.at[k], list_recv.at[k], device)
+        for k, (src, there, device) in enumerate(
+            (
+                (far_src, source_in, holder),
+                (far_type, type_in, holder),
+                (far_src, source_edge, partner),
+                (far_type, type_edge, partner),
+            )
+        )
+    ]
+    for copy in halos + lists:
         copy.start()
 
-    for c in range(OCT_DEV):
-        source = hot(iota((OCTANTS, FAR_K), 0) == far_src[c : c + 1, :])
-        kind_hot = hot(iota((FTYPES, FAR_K), 0) == far_type[c : c + 1, :])
-        far_count[c * FTYPES : (c + 1) * FTYPES, :] = dot(kind_hot, source, 1, 1).astype(BF)
+    for copy in loads[6:9]:
+        copy.wait()
+    listed = near_list[...]
+    inside = (listed >= HALO) & (listed < HALO + LEAF)
+    spot = jnp.where(inside, listed - HALO, jnp.where(listed < HALO, listed + LEAF, listed))
+    kind = near_type[...]
+    one = jnp.ones_like(kind)
+    first_word = jnp.where(kind < 4, one << (8 * jnp.minimum(kind, 3)), 0)
+    other_word = jnp.where(
+        (kind >= 4) & (kind < NTYPES), one << (8 * (jnp.clip(kind, 4, 7) - 4)), 0
+    )
+    slots[0] = spot
+    slots[1] = first_word
+    slots[2] = other_word
+
+    def count_rows(block, carry):
+        base = pl.multiple_of(block * 32, 32)
+        place_of = iota((32, LEAF), 0) + base
+        first = jnp.zeros((32, LEAF), I32)
+        other = jnp.zeros((32, LEAF), I32)
+        for k in range(NEAR_K):
+            here = place_of == slots[0, k : k + 1, :]
+            first = first + jnp.where(here, slots[1, k : k + 1, :], 0)
+            other = other + jnp.where(here, slots[2, k : k + 1, :], 0)
+        for t in range(NTYPES):
+            word = first if t < 4 else other
+            value = lax.shift_right_logical(word, jnp.full_like(word, 8 * (t % 4))) & 255
+            lanes = slice((t % 2) * LEAF, (t % 2 + 1) * LEAF)
+            counts[t // 2, pl.ds(base, 32), lanes] = value.astype(F32).astype(BF)
+        return carry
+
+    lax.fori_loop(0, 16, count_rows, 0)
+
+    all_line = remote(
+        poles.at[pl.ds(0, LINE - 1)], poles.at[pl.ds(0, LINE - 1)], line_send, line_recv, partner
+    )
+    all_line.wait_recv()
+    line = poles.at[pl.ds(grp * SEG + (seg // LINE) * LINE, LINE)]
+
+    def send_line(j, carry):
+        remote(line, line, plane_send, plane_recv, in_plane(j)).start()
+        return carry
+
+    lax.fori_loop(1, PLANE, send_line, 0)
 
     owner_row = new_owner[...].astype(F32)
     leaf_row = iota((LEAF, LEAF), 0)
@@ -230,13 +290,32 @@
     target = (owner_row * float(CAP) + rank).astype(I32)
     place[...] = hot(iota((DEV * CAP, LEAF), 0) == target)
 
+    for copy in lists:
+        copy.wait_recv()
+    even = lax.rem(jnp.full((1, FAR_K), me, I32), 2) == 0
+    lane = iota((FTYPES, OCTANTS), 1)
+    for c in range(9):
+        if c < OCT_DEV:
+            source, kind_row = source_in[c : c + 1, :], type_in[c : c + 1, :]
+        else:
+            source = jnp.where(even, far_src[0:1, :], source_edge[0:1, :])
+            kind_row = jnp.where(even, far_type[0:1, :], type_edge[0:1, :])
+        source_hot = hot(iota((OCTANTS, FAR_K), 0) == source)
+        kind_hot = hot(iota((FTYPES, FAR_K), 0) == kind_row)
+        number = dot(kind_hot, source_hot, 1, 1)
+        first = jnp.where(lax.rem(lane, 8) == 0, pltpu.roll(number, OCTANTS - 8, 1), 0.0)
+        second = jnp.where(lax.rem(lane, 8) == 1, pltpu.roll(number, OCTANTS - 7, 1), 0.0)
+        for k, value in enumerate((number, first, second)):
+            at = k * TARGETS + c * FTYPES
+            far_count[at : at + FTYPES, :] = value.astype(BF)
+
     raw_ops[rows : NBLK * 256, :] = jnp.zeros((NBLK * 256 - rows, COEF), BF)
     for t in range(NTYPES):
         ops[:, t * KPAD + 768 : (t + 1) * KPAD] = jnp.zeros((NBLK * OBLK, 128), BF)
         group[t * KPAD + 848 : (t + 1) * KPAD, :] = jnp.zeros((48, LEAF), BF)
     turn_row = iota((256, 256), 0)
     turn = hot(iota((256, 256), 1) == lax.rem(turn_row, OBLK) * NTYPES + turn_row // OBLK)
-    for copy in loads[9:12]:
+    for copy in loads[9:11]:
         copy.wait()
 
     def turn_blocks(b, carry):
@@ -249,47 +328,32 @@
                 ops[out_rows, t * KPAD : t * KPAD + COEF] = turned[t * OBLK : (t + 1) * OBLK, :]
         return carry
 
-    lax.fori_loop(0, 6, turn_blocks, 0)
-
-    many = pl.ds(0, SEG - 1)
-    all_poles = remote(poles.at[many], poles.at[many], pole_send, pole_recv, partner)
-    all_poles.wait_recv()
+    for k, copy in enumerate(chunks):
+        copy.wait()
+        turn_blocks(k, 0)
+
+    rest_of = pl.ds(0, SEG - LINE)
+    all_plane = remote(poles.at[rest_of], poles.at[rest_of], plane_send, plane_recv, partner)
+    all_plane.wait_recv()
     mine = poles.at[pl.ds(grp * SEG, SEG)]
     pair = remote(mine, mine, pair_send, pair_recv, partner)
     pair.start()
-    lax.fori_loop(6, 9, turn_blocks, 0)
 
     for copy in halos:
         copy.wait_recv()
 
-    def gather_kinds(pair_of, carry):
-        for part in range(2):
-            t = pair_of * 2 + part
-            base = pl.multiple_of(t * KPAD, KPAD)
-            group[pl.ds(base, COEF), :] = dot(window[...], counts[t]).astype(BF)
-            mixed[t] = dot(tracers[...], counts[t])
-        return carry
-
-    lax.fori_loop(0, NTYPES // 2, gather_kinds, 0)
-
-    pair.wait_recv()
-    every = poles[...].astype(F32)
-    edge_pole = every[:, 8:9, :]
-    moved_edge = jnp.concatenate([jnp.zeros((1, 1, 256), F32), edge_pole[: DEV - 1]], axis=0)
-    octant_pole = every[:, 0:8, :] + jnp.where(iota((DEV, 8, 256), 1) == 0, moved_edge, 0.0)
-    octant_pole = octant_pole.reshape(OCTANTS, 256).astype(BF)
-    grouped = dot(far_count[...], octant_pole).astype(BF)[:, 0:MULT]
-    shifted = dot(far_ops[...], grouped, 1, 1).reshape(MULT, FTYPES, 128)
-    same = lax.rem(iota((1, FTYPES, 128), 2), FTYPES) == iota((1, FTYPES, 128), 1)
-    by_kind = jnp.sum(jnp.where(same, shifted, 0.0), axis=1).astype(BF)
-    fold = hot(iota((16, 128), 1) // FTYPES == iota((16, 128), 0))
-    local_own[...] = jnp.zeros((16, 256), BF)
-    local_own[:, 0:MULT] = dot(fold, by_kind, 1, 1).astype(BF)
-    holder = jnp.where(lax.rem(me, 2) == 0, me + 1, lax.rem(me + SEG + 1, DEV))
-    to_holder = remote(local_own, local_in, local_send.at[0], local_recv.at[0], holder)
-    to_holder.start()
-    to_pair = remote(local_own, local_edge, local_send.at[1], local_recv.at[1], partner)
-    to_pair.start()
+    def gather_kinds(two, carry):
+        base = two * 2 * KPAD
+        total = dot(window[...], counts[two]).astype(BF)
+        group[pl.ds(base, COEF), :] = total[:, 0:LEAF]
+        group[pl.ds(base + KPAD, COEF), :] = total[:, LEAF : 2 * LEAF]
+        blend = dot(tracers[...], counts[two])
+        mixed[two * 2, 0:NCOEF, :] = blend[:, 0:LEAF]
+        mixed[two * 2 + 1, 0:NCOEF, :] = blend[:, LEAF : 2 * LEAF]
+        return carry
+
+    for two in range(NTYPES // 2):
+        gather_kinds(two, 0)
 
     def near_rows(block, carry):
         here = pl.ds(pl.multiple_of(block * 320, 32), 320)
@@ -298,16 +362,24 @@
 
     lax.fori_loop(0, 2, near_rows, 0)
 
-    to_holder.wait_recv()
-    to_pair.wait_recv()
-    row = iota((16, 256), 0)
-    from_own = local_own[...].astype(F32)[0:1, :]
-    from_pair = local_edge[...].astype(F32)[0:1, :]
-    even = lax.rem(jnp.full((1, 256), me, I32), 2) == 0
-    ninth = jnp.where(even, from_own, from_pair)
-    nine = jnp.where(row < 8, local_in[...].astype(F32), jnp.where(row == 8, ninth, 0.0))
-    leaf_local = dot(nine.astype(BF)[:, 0:MULT], piece, 0, 0).astype(BF)
-    velocity[0:FRONT, :] = velocity[0:FRONT, :] + dot(down_op[:, 0:FRONT], leaf_local, 0, 0)
+    pair.wait_recv()
+    every = poles[...].astype(F32).reshape(OCTANTS, 256).astype(BF)
+    sums = dot(far_count[...], every)
+    lane = iota((TARGETS, 256), 1)
+    first = pltpu.roll(sums[TARGETS : 2 * TARGETS], 256 - MULT, 1)
+    second = pltpu.roll(sums[2 * TARGETS : 3 * TARGETS], 256 - CUT_BACK, 1)
+    extra = jnp.where(lane < CUT, first, jnp.where(lane < MULT, second, 0.0))
+    grouped = (sums[0:TARGETS] + extra).astype(BF)[:, 0:MULT]
+    shifted = dot(far_ops[...], grouped, 1, 1)
+    far_row = iota((MULT * FTYPES, TARGETS), 0)
+    same = lax.rem(iota((MULT * FTYPES, TARGETS), 1), FTYPES) == lax.rem(far_row, FTYPES)
+    shifted = jnp.where(same, shifted, 0.0).astype(BF)
+    kinds = hot(iota((MULT, MULT * FTYPES), 1) // FTYPES == iota((MULT, MULT * FTYPES), 0))
+    by_kind = dot(kinds, shifted).astype(BF)
+    fold = hot(iota((16, TARGETS), 1) // FTYPES == iota((16, TARGETS), 0))
+    nine = dot(fold, by_kind, 1, 1).astype(BF)
+    leaf_local = dot(nine, piece, 0, 0).astype(BF)
+    velocity[...] = velocity[...] + dot(down_op[:, 0:FRONT], leaf_local, 0, 0)
 
     message = dot(place[...], velocity[0:FRONT, :].astype(BF), 1, 1)
     front[...] = message.reshape(DEV, CAP, FRONT).astype(BF)
@@ -340,7 +412,7 @@
     for t, (flow, number) in enumerate(flows):
         weight = flow / denominator
         kept = kept - weight * number
-        blended = blended + mixed[t] * weight
+        blended = blended + mixed[t, 0:NCOEF, :] * weight
     blended = blended + tracers[:, 0:LEAF].astype(F32) * kept
 
     lower = jnp.concatenate([rest, blended, jnp.zeros((BACK - REST, LEAF), F32)], axis=0)
@@ -356,12 +428,11 @@
     arrived_front[pl.ds(me, 1)] = front[pl.ds(me, 1)]
     arrived_back[pl.ds(me, 1)] = back[pl.ds(me, 1)]
 
-    for copy in halos:
+    for copy in halos + lists:
         copy.wait_send()
-    all_poles.wait_send()
+    all_line.wait_send()
+    all_plane.wait_send()
     pair.wait_send()
-    to_holder.wait_send()
-    to_pair.wait_send()
     most = pl.ds(0, DEV - 1)
     for k, (sent, got) in enumerate(((front, arrived_front), (back, arrived_back))):
         last = remote(sent.at[most], got.at[most], move_send.at[k], move_recv.at[k], partner)
@@ -411,28 +482,31 @@
             VMEM((1, LEAF), I32),
             VMEM((NBLK * 256, COEF), BF),
             VMEM((NBLK * OBLK, NTYPES * KPAD), BF),
-            VMEM((NTYPES, 2 * LEAF, LEAF), BF),
+            VMEM((NTYPES // 2, 2 * LEAF, 2 * LEAF), BF),
             VMEM((NTYPES * KPAD, LEAF), BF),
-            VMEM((NTYPES, NCOEF, LEAF), F32),
-            VMEM((DEV, 16, 256), BF),
-            VMEM((128, OCTANTS), BF),
-            VMEM((16, 256), BF),
-            VMEM((16, 256), BF),
-            VMEM((16, 256), BF),
+            VMEM((NTYPES, 288, LEAF), F32),
+            VMEM((DEV, 8, 256), BF),
+            VMEM((3 * TARGETS, OCTANTS), BF),
+            VMEM((OCT_DEV, FAR_K), I32),
+            VMEM((OCT_DEV, FAR_K), I32),
+            VMEM((OCT_DEV, FAR_K), I32),
+            VMEM((OCT_DEV, FAR_K), I32),
             VMEM((DEV * CAP, LEAF), BF),
             VMEM((FRONT, LEAF), F32),
             VMEM((DEV, CAP, FRONT), BF),
             VMEM((DEV, CAP, BACK), BF),
             VMEM((3, NEAR_K, LEAF), I32),
-            dma((12,)),
+            dma((11 + CHUNKS,)),
+            dma((4,)),
+            dma((4,)),
             dma((4,)),
             dma((4,)),
             dma,
             dma,
             dma,
             dma,
-            dma((2,)),
-            dma((2,)),
+            dma,
+            dma,
             dma((2,)),
             dma((2,)),
         ],

time: 55.6 us -> 54.6 us (0.982)
  Pallas kernels: 55.5 us -> 54.4 us
    pallas_call x1, Pallas kernels: 52.8 us -> 51.7 us  [step(): pl.pallas_call(step_kernel, name='step', out_shape=(jax.ShapeDtypeStruct(...]
where the time goes in v3:
time: 54.6 us; the launch traced here: 54.4 us
  Pallas kernels  54.4 us (100%)
    pallas_call x1, Pallas kernels, step(): pl.pallas_call(step_kernel, name='step', out_shape=(jax.ShapeDtypeStruct(...  51.7 us
    pallas_call x1, Pallas kernels, local(): pl.pallas_call(turn_kernel, name='turn', out_shape=jax.ShapeDtypeStruct((...  2.66 us

profile of v3, /device:TPU:1, one launch (start us, length us, event | category | flops | bytes accessed | tf_op | source)
XLA Modules:
  0.0 54.4 jit_solution(16352427626615126814)
XLA Ops:
  0.0 51.7 %step.1 = (bf16[128,4,640]{2,1,0:T(4,128)(2,1)}, bf16[128,4,512]{2,1,0:T(4,128)(2,1)}) custom-call(bf16[858,256]{1,0:T(8,128)(2,1)} %coeffs_hbm.1, bf16[286,256]{1,0:T(8,128)(2,1)} %tracer_hbm.1, bf16[168,858]{1,0:T(8,128)(2,1)} %up_hbm.1, bf16[2688,168]{1,0:T(8,128)(2,1)} %bitcast.8, bf16[168,858]{1,0:T(8,128)(2,1)} %bitcast.9, bf16[6864,858]{1,0:T(8,128)(2,1)} %bitcast.7, ...), custom_call_target="tpu_custom_call" | custom-call | tf_op jit(solution)/shard_map/step/pallas_call | solution.py:462
  51.7 2.7 %turn.1 = bf16[1144,512]{1,0:T(8,128)(2,1)} custom-call(bf16[128,4,640]{2,1,0:T(4,128)(2,1)} %get-tuple-element.7.front, bf16[128,4,512]{2,1,0:T(4,128)(2,1)} %get-tuple-element.8.back), custom_call_target="tpu_custom_call" | custom-call | tf_op jit(solution)/shard_map/turn/pallas_call | solution.py:541

commit v4 on v3

--- a/solution.py
+++ b/solution.py
@@ -24,9 +24,9 @@
 KPAD = 896
 OBLK = 32
 NBLK = 27
-FRONT = 640
-BACK = 512
-REST = 504
+PART = 384
+PARTS = 3
+REST = 376
 LINE = 4
 PLANE = 16
 TARGETS = 144
@@ -80,8 +80,9 @@
     list_hbm,
     kind_hbm,
     owner_hbm,
-    arrived_front,
-    arrived_back,
+    arrived_0,
+    arrived_1,
+    arrived_2,
     window,
     tracers,
     up_op,
@@ -106,14 +107,14 @@
     type_edge,
     place,
     velocity,
-    front,
-    back,
+    leaving,
     slots,
     load_sem,
     halo_send,
     halo_recv,
     list_send,
     list_recv,
+    keep_sem,
     line_send,
     line_recv,
     plane_send,
@@ -355,12 +356,7 @@
     for two in range(NTYPES // 2):
         gather_kinds(two, 0)
 
-    def near_rows(block, carry):
-        here = pl.ds(pl.multiple_of(block * 320, 32), 320)
-        velocity[here, :] = dot(ops[here, :], group[...])
-        return carry
-
-    lax.fori_loop(0, 2, near_rows, 0)
+    velocity[0:PART, :] = dot(ops[0:PART, :], group[...])
 
     pair.wait_recv()
     every = poles[...].astype(F32).reshape(OCTANTS, 256).astype(BF)
@@ -379,20 +375,32 @@
     fold = hot(iota((16, TARGETS), 1) // FTYPES == iota((16, TARGETS), 0))
     nine = dot(fold, by_kind, 1, 1).astype(BF)
     leaf_local = dot(nine, piece, 0, 0).astype(BF)
-    velocity[...] = velocity[...] + dot(down_op[:, 0:FRONT], leaf_local, 0, 0)
-
-    message = dot(place[...], velocity[0:FRONT, :].astype(BF), 1, 1)
-    front[...] = message.reshape(DEV, CAP, FRONT).astype(BF)
-
-    def send_front(j, carry):
-        there = lax.rem(me + j, DEV)
-        remote(front.at[there], arrived_front.at[me], move_send.at[0], move_recv.at[0], there).start()
-        return carry
-
-    lax.fori_loop(1, DEV, send_front, 0)
-
-    rest = dot(ops[FRONT : NBLK * OBLK, :], group[...])[0 : COEF - FRONT, :]
-    rest = rest + dot(down_op[:, FRONT:COEF], leaf_local, 0, 0)
+    velocity[0:PART, :] = velocity[0:PART, :] + dot(down_op[:, 0:PART], leaf_local, 0, 0)
+
+    arrived = (arrived_0, arrived_1, arrived_2)
+    kept_here = []
+
+    def send_part(k, value):
+        message = dot(place[...], value.astype(BF), 1, 1)
+        leaving[k] = message.reshape(DEV, CAP, PART).astype(BF)
+
+        def send_one(j, carry):
+            there = lax.rem(me + j, DEV)
+            here = leaving.at[k, there]
+            remote(here, arrived[k].at[me], move_send.at[k], move_recv.at[k], there).start()
+            return carry
+
+        lax.fori_loop(1, DEV, send_one, 0)
+        copy = pltpu.make_async_copy(leaving.at[k, me], arrived[k].at[me], keep_sem.at[k])
+        copy.start()
+        kept_here.append(copy)
+
+    send_part(0, velocity[0:PART, :])
+    more = dot(ops[PART : 2 * PART, :], group[...])
+    velocity[PART:, :] = more + dot(down_op[:, PART : 2 * PART], leaf_local, 0, 0)
+    send_part(1, velocity[PART:, :])
+    rest = dot(ops[2 * PART : NBLK * OBLK, :], group[...])[0 : COEF - 2 * PART, :]
+    rest = rest + dot(down_op[:, 2 * PART : COEF], leaf_local, 0, 0)
 
     flows = []
     total_in = jnp.zeros((1, LEAF), F32)
@@ -415,18 +423,7 @@
         blended = blended + mixed[t, 0:NCOEF, :] * weight
     blended = blended + tracers[:, 0:LEAF].astype(F32) * kept
 
-    lower = jnp.concatenate([rest, blended, jnp.zeros((BACK - REST, LEAF), F32)], axis=0)
-    message = dot(place[...], lower.astype(BF), 1, 1)
-    back[...] = message.reshape(DEV, CAP, BACK).astype(BF)
-
-    def send_back(j, carry):
-        there = lax.rem(me + j, DEV)
-        remote(back.at[there], arrived_back.at[me], move_send.at[1], move_recv.at[1], there).start()
-        return carry
-
-    lax.fori_loop(1, DEV, send_back, 0)
-    arrived_front[pl.ds(me, 1)] = front[pl.ds(me, 1)]
-    arrived_back[pl.ds(me, 1)] = back[pl.ds(me, 1)]
+    send_part(2, jnp.concatenate([rest, blended, jnp.zeros((PART - REST, LEAF), F32)], axis=0))
 
     for copy in halos + lists:
         copy.wait_send()
@@ -434,8 +431,10 @@
     all_plane.wait_send()
     pair.wait_send()
     most = pl.ds(0, DEV - 1)
-    for k, (sent, got) in enumerate(((front, arrived_front), (back, arrived_back))):
-        last = remote(sent.at[most], got.at[most], move_send.at[k], move_recv.at[k], partner)
+    for k in range(PARTS):
+        kept_here[k].wait()
+        sent, got = leaving.at[k, most], arrived[k].at[most]
+        last = remote(sent, got, move_send.at[k], move_recv.at[k], partner)
         last.wait_send()
         last.wait_recv()
 
@@ -456,18 +455,14 @@
         near_type,
         new_owner,
     ) = args
-    whole = pl.BlockSpec(memory_space=VMEM)
     anywhere = pl.BlockSpec(memory_space=pl.ANY)
     dma = pltpu.SemaphoreType.DMA
     return pl.pallas_call(
         step_kernel,
         name="step",
-        out_shape=(
-            jax.ShapeDtypeStruct((DEV, CAP, FRONT), BF),
-            jax.ShapeDtypeStruct((DEV, CAP, BACK), BF),
-        ),
+        out_shape=(jax.ShapeDtypeStruct((DEV, CAP, PART), BF),) * PARTS,
         in_specs=[anywhere] * 6 + [pl.BlockSpec(memory_space=pltpu.SMEM)] + [anywhere] * 6,
-        out_specs=(whole, whole),
+        out_specs=(anywhere,) * PARTS,
         scratch_shapes=[
             VMEM((COEF, 2 * LEAF), BF),
             VMEM((NCOEF, 2 * LEAF), BF),
@@ -492,23 +487,23 @@
             VMEM((OCT_DEV, FAR_K), I32),
             VMEM((OCT_DEV, FAR_K), I32),
             VMEM((DEV * CAP, LEAF), BF),
-            VMEM((FRONT, LEAF), F32),
-            VMEM((DEV, CAP, FRONT), BF),
-            VMEM((DEV, CAP, BACK), BF),
+            VMEM((2 * PART, LEAF), F32),
+            VMEM((PARTS, DEV, CAP, PART), BF),
             VMEM((3, NEAR_K, LEAF), I32),
             dma((11 + CHUNKS,)),
             dma((4,)),
             dma((4,)),
             dma((4,)),
             dma((4,)),
+            dma((PARTS,)),
             dma,
             dma,
             dma,
             dma,
             dma,
             dma,
-            dma((2,)),
-            dma((2,)),
+            dma((PARTS,)),
+            dma((PARTS,)),
         ],
         compiler_params=pltpu.CompilerParams(
             collective_id=0, has_side_effects=True, vmem_limit_bytes=67_043_328
@@ -530,18 +525,41 @@
     )
 
 
-def turn_kernel(front, back, moved):
-    slots = DEV * CAP
-    moved[0:FRONT, :] = front[...].astype(F32).reshape(slots, FRONT).T.astype(BF)
-    turned = back[...].astype(F32).reshape(slots, BACK).T
-    moved[FRONT : COEF + NCOEF, :] = turned[0:REST].astype(BF)
+def turn_kernel(first, second, third, moved, held, turned, in_sem, out_sem):
+    loads = [
+        pltpu.make_async_copy(source, held.at[k], in_sem.at[k])
+        for k, source in enumerate((first, second, third))
+    ]
+    for copy in loads:
+        copy.start()
+    stores = []
+    for k, copy in enumerate(loads):
+        copy.wait()
+        turned[k] = held[k].astype(F32).reshape(DEV * CAP, PART).T.astype(BF)
+        count = PART if k < 2 else REST
+        store = pltpu.make_async_copy(
+            turned.at[k, pl.ds(0, count)], moved.at[pl.ds(k * PART, count)], out_sem.at[k]
+        )
+        store.start()
+        stores.append(store)
+    for copy in stores:
+        copy.wait()
 
 
 def local(*args):
+    anywhere = pl.BlockSpec(memory_space=pl.ANY)
     return pl.pallas_call(
         turn_kernel,
         name="turn",
         out_shape=jax.ShapeDtypeStruct((COEF + NCOEF, DEV * CAP), BF),
+        in_specs=[anywhere] * PARTS,
+        out_specs=anywhere,
+        scratch_shapes=[
+            VMEM((PARTS, DEV, CAP, PART), BF),
+            VMEM((PARTS, PART, DEV * CAP), BF),
+            pltpu.SemaphoreType.DMA((PARTS,)),
+            pltpu.SemaphoreType.DMA((PARTS,)),
+        ],
     )(*step(*args))
 
 

time: 54.6 us -> 54.7 us (level)
  no operation moved by 1% of the time
where the time goes in v4:
time: 54.7 us; the launch traced here: 54.5 us
  Pallas kernels  54.4 us (99%)
    pallas_call x1, Pallas kernels, step(): pl.pallas_call(step_kernel, name='step', out_shape=(jax.ShapeDtypeStruct(...  52.1 us
    pallas_call x1, Pallas kernels, local(): pl.pallas_call(turn_kernel, name='turn', out_shape=jax.ShapeDtypeStruct((...  2.32 us

profile of v4, /device:TPU:1, one launch (start us, length us, event | category | flops | bytes accessed | tf_op | source)
XLA Modules:
  0.0 54.5 jit_solution(976587841749311817)
XLA Ops:
  0.0 52.1 %step.1 = (bf16[128,4,384]{2,1,0:T(4,128)(2,1)}, bf16[128,4,384]{2,1,0:T(4,128)(2,1)}, bf16[128,4,384]{2,1,0:T(4,128)(2,1)}) custom-call(bf16[858,256]{1,0:T(8,128)(2,1)} %coeffs_hbm.1, bf16[286,256]{1,0:T(8,128)(2,1)} %tracer_hbm.1, bf16[168,858]{1,0:T(8,128)(2,1)} %up_hbm.1, bf16[2688,168]{1,0:T(8,128)(2,1)} %bitcast.8, bf16[168,858]{1,0:T(8,128)(2,1)} %bitcast.9, ...), custom_call_target="tpu_custom_call" | custom-call | tf_op jit(solution)/shard_map/step/pallas_call | solution.py:460
  52.1 2.3 %turn.1 = bf16[1144,512]{1,0:T(8,128)(2,1)} custom-call(bf16[128,4,384]{2,1,0:T(4,128)(2,1)} %get-tuple-element.8.first, bf16[128,4,384]{2,1,0:T(4,128)(2,1)} %get-tuple-element.9.second, bf16[128,4,384]{2,1,0:T(4,128)(2,1)} %get-tuple-element.10.third), custom_call_target="tpu_custom_call" | custom-call | tf_op jit(solution)/shard_map/turn/pallas_call | solution.py:551
